TPU v7x, 512 devices: a whole 4x8x8 slice. The times are simulated.
512 devices in a mesh: member: 16 (over x, y_hi, core), tile: 32 (over y_lo, z).
Axes of the slice: x: 4, y: 8 (y_hi: 2, y_lo: 4; y = y_hi * 4 + y_lo), z: 8, core: 2. Of those that a mesh axis runs over, the one named last changes fastest.
Arguments:
- states: bfloat16 [16, 8, 2048, 2048], P('member', None, 'tile'), may hold values from -8 to 8
- obs_var: float32 [8], replicated, may hold values from 2 to 30
- relax_rate: float32 [8], replicated, may hold values from 0.3 to 1
Outputs:
- nudged: bfloat16 [16, 8, 2048, 2048], P('member', None, 'tile')
- spread: float32 [8, 256, 256], P(None, 'tile')
All inputs are finite; a program needn't handle non-finite values.
Results may differ from a plain program's by a relative error of at most 0.0034.
Values may be sent and summed in bfloat16 or wider, within the bound.
No kernel may reach another device: no remote copies, remote signals or barrier semaphores. Data moves between devices by JAX's collectives and lax.ppermute only.
A program may use at most 64 MiB of HBM per device.

v0:
```python
import math

import jax
import jax.numpy as jnp
from jax import lax
from jax.sharding import PartitionSpec as P

NX = 2048
MODES = 256


def copy_for_each(shard, axis):
    copies = jnp.broadcast_to(shard, (lax.axis_size(axis), *shard.shape))
    return lax.all_to_all(copies, axis, split_axis=0, concat_axis=0, tiled=True)


def taken_together(shard, axis):
    everything = copy_for_each(shard, axis)
    return jnp.sum(everything, axis=0)


def in_one(arrays, axis):
    ends = [0]
    for a in arrays:
        ends.append(ends[-1] + a.size)
    running = taken_together(jnp.concatenate([a.ravel() for a in arrays]), axis)
    return tuple((running[b:e].reshape(a.shape) for a, b, e in zip(arrays, ends, ends[1:])))


def mode_table(positions, extent, mode_count):
    mode_index = jnp.arange(mode_count, dtype=jnp.int32)[None, :]
    wavenum = (mode_index + 1) // 2
    phases = positions[:, None] * wavenum % extent
    angles = 2.0 * math.pi / extent * phases.astype(jnp.float32)
    scaled = jnp.where(mode_index % 2 == 1, jnp.sin(angles), jnp.cos(angles))
    factor = jnp.where(mode_index == 0, math.sqrt(1.0 / extent), math.sqrt(2.0 / extent))
    return scaled * factor


def per_device(states, obs_var, relax_rate):
    layer_field = states[0]
    levels, row_count, col_count = layer_field.shape
    by_half = mode_table(jnp.arange(col_count, dtype=jnp.int32), col_count, MODES).astype(
        jnp.bfloat16
    )
    projected = jnp.dot(
        layer_field.reshape(levels * row_count, col_count),
        by_half,
        preferred_element_type=jnp.float32,
    )
    projected = projected.reshape(levels, row_count, MODES)
    table_full = mode_table(jnp.arange(NX, dtype=jnp.int32), NX, MODES)
    gathered_rows = lax.all_to_all(projected, "tile", split_axis=2, concat_axis=1, tiled=True)
    item_count, full_rows, block_cols = gathered_rows.shape
    flat_rows = jnp.transpose(gathered_rows, (1, 0, 2)).reshape(full_rows, item_count * block_cols)
    product = jnp.dot(
        table_full.T, flat_rows, precision=lax.Precision.HIGHEST, preferred_element_type=jnp.float32
    )
    product = jnp.transpose(product.reshape(MODES, item_count, block_cols), (1, 0, 2))
    coeffs = lax.all_to_all(product, "tile", split_axis=1, concat_axis=2, tiled=True)
    members = lax.axis_size("member")
    owner_mask = (lax.axis_index("member") == 0).astype(jnp.float32)
    totals, driver = in_one((coeffs, coeffs * owner_mask), "member")
    centered = coeffs - totals / members
    spread = taken_together(centered * centered, "member") / members
    departure = coeffs - driver
    weight_gain = relax_rate[:, None, None] * spread / (spread + obs_var[:, None, None])
    misfit = -weight_gain * departure
    misfit_cols = lax.all_to_all(misfit, "tile", split_axis=2, concat_axis=1, tiled=True)
    block_cols = misfit_cols.shape[2]
    flat_misfit = jnp.transpose(misfit_cols, (1, 0, 2)).reshape(MODES, levels * block_cols)
    wide_flat = jnp.dot(
        table_full, flat_misfit, precision=lax.Precision.HIGHEST, preferred_element_type=jnp.float32
    )
    wide_rows = jnp.transpose(wide_flat.reshape(NX, levels, block_cols), (1, 0, 2)).astype(
        jnp.bfloat16
    )
    rows_back = lax.all_to_all(wide_rows, "tile", split_axis=1, concat_axis=2, tiled=True)
    increment = jnp.dot(
        rows_back.reshape(levels * row_count, MODES), by_half.T, preferred_element_type=jnp.float32
    )
    increment = increment.reshape(levels, row_count, col_count)
    nudged = (layer_field.astype(jnp.float32) + increment).astype(jnp.bfloat16)
    return (nudged[None], spread)


def solution(mesh):
    in_specs = (P("member", None, "tile", None), P(), P())
    out_specs = (P("member", None, "tile", None), P(None, "tile", None))
    return jax.shard_map(
        per_device, mesh=mesh, in_specs=in_specs, out_specs=out_specs, check_vma=False
    )
```

profile of v0, /device:TPU:1, one launch (start us, length us, event | category | flops | bytes accessed | tf_op | source)
XLA Modules:
  0.0 251.4 jit_solution(14586560933564707945)
XLA Ops:
  0.7 11.3 %convolution_bitcast_fusion = f32[512,256]{0,1:T(8,128)S(1)} fusion(bf16[512,2048]{1,0:T(8,128)(2,1)} %bitcast.89, f32[256]{0:T(256)S(1)} %compare_select_fusion, s32[256]{0:T(256)S(1)} %and_select_fusion, pred[256]{0:T(512)(128)(4,1)S(1)} %fusion.22), kind=kOutput, calls=%fused_computation.18 | convolution fusion | flops 545783808 | bytes 2623744 | tf_op jit(solution)/shard_map/dot_general | solution.py:46
  12.0 0.2 copy.50
  12.2 0.4 copy.51
  12.6 0.7 reshape.125
  13.3 29.1 %all_to_all.80 = f32[32,1,4096]{2,1,0:T(1,128)S(1)} all-to-all(f32[32,1,4096]{2,1,0:T(1,128)S(1)} %reshape.125), channel_id=1, replica_groups=mesh['member'=16,'tile'=32] {'tile'}, dimensions={0} | all-to-all | bytes 1048576 | tf_op jit(solution)/shard_map/all_to_all | solution.py:53
  42.3 0.6 broadcast.153
  42.9 1.9 reduce.1
  44.9 0.4 reshape.126
  45.3 0.6 copy.53
  45.9 0.4 all_to_all.60
  46.3 9.9 %fusion.12 = f32[8,256,8]{1,2,0:T(8,128)S(1)} fusion(f32[256]{0:T(256)S(1)} %compare_select_fusion, s32[256]{0:T(256)S(1)} %and_select_fusion, pred[256]{0:T(512)(128)(4,1)S(1)} %fusion.22, f32[8,2048,8]{1,2,0:T(8,128)S(1)} %all_to_all.60), kind=kOutput, calls=%fused_computation.19 | convolution fusion | flops 411041792 | bytes 592128 | tf_op jit(solution)/shard_map/dot_general | solution.py:56
  56.2 0.4 copy.54
  56.6 1.2 reshape.127
  57.8 7.3 %all-to-all-start.1 = ((f32[32,1,512]{2,1,0:T(1,128)}), f32[32,1,512]{2,1,0:T(1,128)S(1)}, u32[]{:S(2)}, u32[]{:S(2)}) async-start(f32[32,1,512]{2,1,0:T(1,128)} %reshape.127), calls=%async_computation.1 | async-start | bytes 131072 | tf_op jit(solution)/shard_map/all_to_all | solution.py:60
  65.1 9.1 %all-to-all-done.1 = f32[32,1,512]{2,1,0:T(1,128)S(1)} async-done(((f32[32,1,512]{2,1,0:T(1,128)}), f32[32,1,512]{2,1,0:T(1,128)S(1)}, u32[]{:S(2)}, u32[]{:S(2)}) %all-to-all-start.1) | async-done | bytes 65568 | tf_op jit(solution)/shard_map/all_to_all | solution.py:60
  74.2 0.8 reduce.2
  75.1 0.6 reshape.128
  75.6 0.6 copy.56
  76.3 0.5 reshape.120
  76.8 2.9 %broadcast_in_dim.45 = f32[16,1,32768]{2,1,0:T(1,128)} broadcast(f32[32768]{0:T(1024)S(1)} %pad_maximum_fusion), dimensions={2} | broadcast | bytes 2228224 | tf_op jit(solution)/shard_map/broadcast_in_dim | solution.py:13
  79.7 8.8 %all-to-all-start.2 = ((f32[16,1,32768]{2,1,0:T(1,128)}), f32[16,1,32768]{2,1,0:T(1,128)S(1)}, u32[]{:S(2)}, u32[]{:S(2)}) async-start(f32[16,1,32768]{2,1,0:T(1,128)} %broadcast_in_dim.45), calls=%async_computation.2 | async-start | bytes 4194304 | tf_op jit(solution)/shard_map/all_to_all | solution.py:14
  88.6 0.5 all_to_all.64
  89.1 45.5 %all-to-all-done.2 = f32[16,1,32768]{2,1,0:T(1,128)S(1)} async-done(((f32[16,1,32768]{2,1,0:T(1,128)}), f32[16,1,32768]{2,1,0:T(1,128)S(1)}, u32[]{:S(2)}, u32[]{:S(2)}) %all-to-all-start.2) | async-done | bytes 2097184 | tf_op jit(solution)/shard_map/all_to_all | solution.py:14
  134.6 1.4 reduce_sum.18
  136.0 0.0 copy-start.2
  136.0 0.0 copy-start
  136.1 1.1 broadcast_in_dim.46
  137.1 10.2 %all-to-all-start.3 = ((f32[16,8,8,256]{3,2,1,0:T(8,128)}), f32[16,8,8,256]{3,2,1,0:T(8,128)S(1)}, u32[]{:S(2)}, u32[]{:S(2)}) async-start(f32[16,8,8,256]{3,2,1,0:T(8,128)} %broadcast_in_dim.46), calls=%async_computation.3 | async-start | bytes 2097152 | tf_op jit(solution)/shard_map/all_to_all | solution.py:14
  147.3 0.0 copy-done.2
  147.4 21.0 %all-to-all-done.3 = f32[16,8,8,256]{3,2,1,0:T(8,128)S(1)} async-done(((f32[16,8,8,256]{3,2,1,0:T(8,128)}), f32[16,8,8,256]{3,2,1,0:T(8,128)S(1)}, u32[]{:S(2)}, u32[]{:S(2)}) %all-to-all-start.3) | async-done | bytes 1048608 | tf_op jit(solution)/shard_map/all_to_all | solution.py:14
  168.4 0.1 reduce_sum.19
  168.4 0.0 copy-done
  168.4 0.6 subtract_multiply_fusion
  169.1 0.4 copy.59
  169.5 0.5 reshape.129
  170.0 22.5 %all_to_all.81 = f32[32,1,512]{2,1,0:T(1,128)S(1)} all-to-all(f32[32,1,512]{2,1,0:T(1,128)S(1)} %reshape.129), channel_id=1, replica_groups=mesh['member'=16,'tile'=32] {'tile'}, dimensions={0} | all-to-all | bytes 131072 | tf_op jit(solution)/shard_map/all_to_all | solution.py:69
  192.5 0.8 reduce.3
  193.4 0.6 reshape.130
  194.0 0.6 copy.61
  194.6 0.5 all_to_all.70
  195.1 11.4 %fusion.2 = bf16[8,2048,8]{1,2,0:T(8,128)(2,1)S(1)} fusion(f32[256]{0:T(256)S(1)} %compare_select_fusion, s32[256]{0:T(256)S(1)} %and_select_fusion, pred[256]{0:T(512)(128)(4,1)S(1)} %fusion.22, f32[8,256,8]{1,2,0:T(8,128)S(1)} %all_to_all.70), kind=kOutput, calls=%fused_computation.7 | convolution fusion | flops 411172864 | bytes 329984 | tf_op jit(solution)/shard_map/dot_general | solution.py:72
  206.6 4.0 %copy.62 = bf16[8,2048,8]{2,0,1:T(8,128)(2,1)} copy(bf16[8,2048,8]{1,2,0:T(8,128)(2,1)S(1)} %fusion.2) | data formatting | bytes 524288 | tf_op jit(solution)/shard_map/convert_element_type | solution.py:75
  210.6 5.8 %reshape.131 = bf16[32,2,2048]{2,1,0:T(2,128)(2,1)S(1)} reshape(bf16[2048,8,8]{2,1,0:T(8,128)(2,1)} %bitcast.80) | data formatting | bytes 524288
  216.4 13.4 %all_to_all.82 = bf16[32,2,2048]{2,1,0:T(2,128)(2,1)S(1)} all-to-all(bf16[32,2,2048]{2,1,0:T(2,128)(2,1)S(1)} %reshape.131), channel_id=1, replica_groups=mesh['member'=16,'tile'=32] {'tile'}, dimensions={0} | all-to-all | bytes 524288 | tf_op jit(solution)/shard_map/all_to_all | solution.py:78
  229.8 5.9 %reshape.132 = bf16[2048,8,8]{2,1,0:T(8,128)(2,1)} reshape(bf16[32,2,2048]{2,1,0:T(2,128)(2,1)S(1)} %all_to_all.82) | data formatting | bytes 524288
  235.7 4.6 %copy.63 = bf16[8,32,64,8]{2,3,1,0:T(8,128)(2,1)S(1)} copy(bf16[8,32,64,8]{3,0,2,1:T(8,128)(2,1)} %bitcast.81) | data formatting | bytes 524288 | tf_op jit(solution)/shard_map/all_to_all | solution.py:78
  240.3 0.0 copy-done.1
  240.3 11.1 %fusion.1 = bf16[1,8,64,2048]{3,2,1,0:T(8,128)(2,1)} fusion(bf16[1,8,64,2048]{3,2,1,0:T(8,128)(2,1)S(1)} %copy-done.1, f32[256]{0:T(256)S(1)} %compare_select_fusion, s32[256]{0:T(256)S(1)} %and_select_fusion, pred[256]{0:T(512)(128)(4,1)S(1)} %fusion.22, bf16[8,32,64,8]{2,3,1,0:T(8,128)(2,1)S(1)} %copy.63), kind=kOutput, calls=%fused_computation.5 | convolution fusion | flops 548929536 | bytes 4458752 | tf_op jit(solution)/shard_map/dot_general | solution.py:79
  (11 shorter events, 0.1 us)
Async XLA Ops:
  57.8 16.4 %all-to-all-start.1 = ((f32[32,1,512]{2,1,0:T(1,128)}), f32[32,1,512]{2,1,0:T(1,128)S(1)}, u32[]{:S(2)}, u32[]{:S(2)}) async-start(f32[32,1,512]{2,1,0:T(1,128)} %reshape.127), calls=%async_computation.1 | async-start | bytes 131072 | tf_op jit(solution)/shard_map/all_to_all | solution.py:60
  79.7 54.8 %all-to-all-start.2 = ((f32[16,1,32768]{2,1,0:T(1,128)}), f32[16,1,32768]{2,1,0:T(1,128)S(1)}, u32[]{:S(2)}, u32[]{:S(2)}) async-start(f32[16,1,32768]{2,1,0:T(1,128)} %broadcast_in_dim.45), calls=%async_computation.2 | async-start | bytes 4194304 | tf_op jit(solution)/shard_map/all_to_all | solution.py:14
  136.0 11.4 %copy-start.2 = (f32[8]{0:T(128)S(1)}, f32[8]{0:T(128)}, u32[]{:S(2)}) copy-start(f32[8]{0:T(128)} %param.5) | copy-start | bytes 100
  136.0 32.4 %copy-start = (f32[8]{0:T(128)S(1)}, f32[8]{0:T(128)}, u32[]{:S(2)}) copy-start(f32[8]{0:T(128)} %param.4) | copy-start | bytes 100
  137.1 31.2 %all-to-all-start.3 = ((f32[16,8,8,256]{3,2,1,0:T(8,128)}), f32[16,8,8,256]{3,2,1,0:T(8,128)S(1)}, u32[]{:S(2)}, u32[]{:S(2)}) async-start(f32[16,8,8,256]{3,2,1,0:T(8,128)} %broadcast_in_dim.46), calls=%async_computation.3 | async-start | bytes 2097152 | tf_op jit(solution)/shard_map/all_to_all | solution.py:14
  235.7 4.6 %copy-start.1 = (bf16[1,8,64,2048]{3,2,1,0:T(8,128)(2,1)S(1)}, bf16[1,8,64,2048]{3,2,1,0:T(8,128)(2,1)}, u32[]{:S(2)}) copy-start(bf16[1,8,64,2048]{3,2,1,0:T(8,128)(2,1)} %param.3) | copy-start | bytes 6291460
where the time goes:
time: 252 us; the launch traced here: 251 us
  waiting for transfers between devices  75.6 us (30%)
  blocking collectives  65 us (26%)
  matrix products  43.7 us (17%)
  local copies, waits for them, and re-layouts  34.1 us (14%)
  starting transfers between devices  26.4 us (10%)
  other arithmetic  5.76 us (2%)
    all_to_all x2, waiting for transfers between devices, copy_for_each(): return lax.all_to_all(copies, axis, split_axis=0, concat_axis=0, tiled=True)  66.4 us
    all_to_all x1, blocking collectives, per_device(): lax.all_to_all(projected, 'tile', split_axis=2, concat_axis=1, tiled=True)  29.1 us
    all_to_all x1, blocking collectives, per_device(): lax.all_to_all(misfit, 'tile', split_axis=2, concat_axis=1, tiled=True)  22.5 us
    all_to_all x2, starting transfers between devices, copy_for_each(): return lax.all_to_all(copies, axis, split_axis=0, concat_axis=0, tiled=True)  19.1 us
    unnamed x14, local copies, waits for them, and re-layouts  15.6 us
    all_to_all x1, blocking collectives, per_device(): lax.all_to_all(wide_rows, 'tile', split_axis=1, concat_axis=2, tiled=True)  13.4 us
    dot_general x1, matrix products, per_device(): jnp.dot(table_full, flat_misfit, precision=lax.Precision.HIGHEST, preferr...  11.4 us
    dot_general x1, matrix products, per_device(): jnp.dot(layer_field.reshape(levels * row_count, col_count), by_half, pref...  11.3 us
  transfers between devices with their start and end apart: 3, of which 3 were waited for; matrix products, arithmetic and copies ran while one was open for 0% of the time, Pallas kernels for 0%

commit v1 on v0

v1 whole, which is shorter than its diff:
```python
import functools
import math

import jax
import jax.numpy as jnp
import numpy as np
from jax import lax
from jax.experimental import pallas as pl
from jax.experimental.pallas import tpu as pltpu
from jax.sharding import Mesh, PartitionSpec as P

N = 2048
MODES = 256
LEVELS = 8
MEMBERS = 16
TILES = 32
ROWS = N // TILES
NEAR = 4
FAR = MEMBERS // NEAR
OWN = MODES // TILES
BF16 = jnp.bfloat16
F32 = jnp.float32


def mode_table():
    mode = np.arange(MODES)[None, :]
    phases = (np.arange(N)[:, None] * ((mode + 1) // 2)) % N
    angles = 2.0 * math.pi / N * phases
    scaled = np.where(mode % 2 == 1, np.sin(angles), np.cos(angles))
    factor = np.where(mode == 0, math.sqrt(1.0 / N), math.sqrt(2.0 / N))
    return (scaled * factor).astype(np.float32)


def tables():
    full = mode_table()
    half = full.astype(BF16)
    first = np.arange(MODES).reshape(TILES, OWN).T.reshape(-1)
    second = np.arange(MODES).reshape(OWN, TILES).T.reshape(-1)
    bx = full[:, first]
    bx_high = bx.astype(BF16)
    bx_low = (bx - bx_high.astype(np.float32)).astype(BF16)
    by = half[:, second]
    return bx_high, bx_low, by, np.ascontiguousarray(by.T)


def dot(a, b, dims):
    return lax.dot_general(a, b, (dims, ((), ())), preferred_element_type=F32)


def project_kernel(states_ref, by_ref, out_ref):
    field = states_ref[...].reshape(2 * ROWS, N)
    half = dot(field, by_ref[...], ((1,), (0,)))
    out_ref[...] = half.T.reshape(TILES, 1, OWN, 2 * ROWS).astype(BF16)


def coeffs_kernel(rows_ref, high_ref, low_ref, out_ref, copies_ref, wide):
    for u in range(TILES // 2):
        a, b = rows_ref[2 * u], rows_ref[2 * u + 1]
        cols = pl.ds(2 * ROWS * u, 2 * ROWS)
        wide[: NEAR * OWN, cols] = jnp.concatenate([a[:, :ROWS], b[:, :ROWS]], axis=1)
        wide[NEAR * OWN :, cols] = jnp.concatenate([a[:, ROWS:], b[:, ROWS:]], axis=1)
    x = wide[...]
    coeffs = dot(x, high_ref[...], ((1,), (0,))) + dot(x, low_ref[...], ((1,), (0,)))
    out_ref[...] = coeffs
    for k in range(FAR):
        copies_ref[k] = coeffs


def nudge_kernel(all_ref, own_ref, obs_ref, relax_ref, high_ref, low_ref, rows_ref, spread_ref):
    pair = lax.axis_index("near")
    spreads, misfits = [], []
    for l in range(2):
        def block(ref, k):
            return ref[pl.ds(NEAR * OWN * l + OWN * k, OWN), :]

        driver = block(all_ref.at[0], 0)
        departures = [
            block(all_ref.at[f], k) - driver for f in range(FAR) for k in range(NEAR)
        ]
        mean = sum(departures[1:], departures[0]) * (1.0 / MEMBERS)
        centered = [d - mean for d in departures]
        squares = [c * c for c in centered]
        spread = sum(squares[1:], squares[0]) * (1.0 / MEMBERS)
        gain = relax_ref[2 * pair + l] * spread / (spread + obs_ref[2 * pair + l])
        spreads.append(spread)
        misfits.extend([-gain * (block(own_ref, k) - driver) for k in range(NEAR)])
    misfit = jnp.concatenate(misfits, axis=0)
    high = misfit.astype(BF16)
    low = (misfit - high.astype(F32)).astype(BF16)
    nt = ((1,), (1,))
    back = dot(high, high_ref[...], nt) + dot(low, high_ref[...], nt) + dot(high, low_ref[...], nt)
    back = back.astype(BF16)
    for u in range(TILES // 2):
        a = back[: NEAR * OWN, 2 * ROWS * u : 2 * ROWS * (u + 1)]
        b = back[NEAR * OWN :, 2 * ROWS * u : 2 * ROWS * (u + 1)]
        rows_ref[2 * u] = jnp.concatenate([a[:, :ROWS], b[:, :ROWS]], axis=1)
        rows_ref[2 * u + 1] = jnp.concatenate([a[:, ROWS:], b[:, ROWS:]], axis=1)
    both = jnp.concatenate(spreads, axis=0)
    stacked = jnp.concatenate([both[:, TILES * k : TILES * (k + 1)] for k in range(OWN)], axis=0)
    flipped = stacked.T
    high = flipped.astype(BF16)
    spread_ref[0] = high
    spread_ref[1] = (flipped - high.astype(F32)).astype(BF16)


def apply_kernel(states_ref, back_ref, parts_ref, by_ref, out_ref, spread_ref, mixed, turned):
    modes = back_ref[...].reshape(MODES, 2 * ROWS)
    increment = dot(modes, by_ref[...], ((0,), (0,)))
    field = states_ref[...].reshape(2 * ROWS, N)
    out_ref[...] = (field.astype(F32) + increment).astype(BF16).reshape(2, ROWS, N)

    @pl.when(pl.program_id(0) == 0)
    def _():
        mixed[...] = parts_ref[0].astype(F32) + parts_ref[1].astype(F32)
        ordered = jnp.concatenate(
            [mixed[pl.ds(c, TILES, stride=NEAR), :] for c in range(NEAR)], axis=0
        )
        turned[...] = ordered.T
        for l in range(2):
            strips = [turned[pl.ds(OWN * l + k, OWN, stride=2 * OWN), :] for k in range(OWN)]
            for c in range(NEAR):
                spread_ref[2 * c + l] = jnp.concatenate(
                    [s[:, TILES * c : TILES * (c + 1)] for s in strips], axis=1
                )


def call(kernel, outs, **kw):
    return pl.pallas_call(
        kernel,
        out_shape=outs,
        compiler_params=pltpu.CompilerParams(vmem_limit_bytes=24 * 1024 * 1024),
        **kw,
    )


def shape(dims, dtype):
    return jax.ShapeDtypeStruct(dims, dtype)


def per_device(consts, states, obs_var, relax_rate):
    bx_high, bx_low, by, by_t = consts
    field = states[0]
    whole = lambda *dims: pl.BlockSpec(dims, lambda i: (0,) * len(dims))
    levels = pl.BlockSpec((2, ROWS, N), lambda i: (i, 0, 0))
    chunks = pl.BlockSpec((TILES, 1, OWN, 2 * ROWS), lambda i: (0, i, 0, 0))
    smem = pl.BlockSpec(memory_space=pltpu.SMEM)
    vmem = pl.BlockSpec(memory_space=pltpu.VMEM)

    sent = call(
        project_kernel,
        shape((TILES, NEAR, OWN, 2 * ROWS), BF16),
        grid=(NEAR,),
        in_specs=[levels, whole(N, MODES)],
        out_specs=chunks,
    )(field, by)
    rows = lax.all_to_all(
        sent.reshape(TILES * NEAR, OWN, 2 * ROWS), ("tile", "near"), 0, 0, tiled=True
    )
    coeffs, copies = call(
        coeffs_kernel,
        (shape((2 * NEAR * OWN, MODES), F32), shape((FAR, 2 * NEAR * OWN, MODES), F32)),
        in_specs=[vmem] * 3,
        out_specs=(vmem, vmem),
        scratch_shapes=[pltpu.VMEM((2 * NEAR * OWN, N), BF16)],
    )(rows.reshape(TILES, NEAR * OWN, 2 * ROWS), bx_high, bx_low)
    gathered = lax.all_to_all(copies, "far", 0, 0, tiled=True)
    back, parts = call(
        nudge_kernel,
        (shape((TILES, NEAR * OWN, 2 * ROWS), BF16), shape((2, TILES, 2 * OWN * OWN), BF16)),
        in_specs=[vmem, vmem, smem, smem, vmem, vmem],
        out_specs=(vmem, vmem),
    )(gathered, coeffs, obs_var, relax_rate, bx_high, bx_low)
    extra = jnp.broadcast_to(
        jnp.transpose(parts, (1, 0, 2))[:, None, None], (TILES, NEAR, 1, 2, 2 * ROWS)
    )
    out = jnp.concatenate([back.reshape(TILES, NEAR, 4, 2, 2 * ROWS), extra], axis=2)
    got = lax.all_to_all(
        out.reshape(TILES * NEAR, 5, 2, 2 * ROWS), ("tile", "near"), 0, 0, tiled=True
    )
    modes = got[:, :4].reshape(TILES, NEAR, OWN, 2 * ROWS)
    parts = jnp.transpose(got[:, 4], (1, 0, 2))
    nudged, spread = call(
        apply_kernel,
        (shape((LEVELS, ROWS, N), BF16), shape((LEVELS, OWN, MODES), F32)),
        grid=(NEAR,),
        in_specs=[levels, chunks, whole(2, TILES * NEAR, 2 * ROWS), whole(MODES, N)],
        out_specs=(levels, whole(LEVELS, OWN, MODES)),
        scratch_shapes=[pltpu.VMEM((2 * ROWS, 2 * ROWS), F32)] * 2,
    )(field, modes, parts, by_t)
    return nudged[None], spread


def solution(mesh):
    fine = Mesh(mesh.devices.reshape(FAR, NEAR, TILES), ("far", "near", "tile"))
    rows = P(("far", "near"), None, "tile", None)
    return jax.shard_map(
        functools.partial(per_device, tables()),
        mesh=fine,
        in_specs=(rows, P(), P()),
        out_specs=(rows, P(None, "tile", None)),
        check_vma=False,
    )
```

time: 252 us -> 76.4 us (0.30)
  waiting for transfers between devices: 75.6 us -> 0 us
  matrix products: 43.7 us -> 0 us
  local copies, waits for them, and re-layouts: 34.1 us -> 3.13 us
  starting transfers between devices: 26.4 us -> 0 us
  Pallas kernels: 0 us -> 6.81 us
  other arithmetic: 5.76 us -> 0.44 us
    all_to_all x3 -> x0, waiting for transfers between devices: 75.6 us -> none  [the longest x2 66.4 us: copy_for_each(): return lax.all_to_all(copies, axis, split_axis=0, concat_axis=0, tiled=True)]
    dot_general x4 -> x0, matrix products: 43.7 us -> none  [the longest x1 11.4 us: per_device(): jnp.dot(table_full, flat_misfit, precision=lax.Precision.HIGHEST, preferr...]
    all_to_all x3 -> x0, starting transfers between devices: 26.4 us -> none  [the longest x2 19.1 us: copy_for_each(): return lax.all_to_all(copies, axis, split_axis=0, concat_axis=0, tiled=True)]
    unnamed x14 -> x17, local copies, waits for them, and re-layouts: 15.6 us -> 2.85 us
    all_to_all x8 -> x0, local copies, waits for them, and re-layouts: 8.49 us -> none  [the longest x1 4.64 us: per_device(): lax.all_to_all(wide_rows, 'tile', split_axis=1, concat_axis=2, tiled=True)]
    pallas_call x0 -> x4, Pallas kernels: none -> 6.81 us  [the longest x1 2.94 us: per_device(): call(apply_kernel, (shape((LEVELS, ROWS, N), BF16), shape((LEVELS, OWN, M...]
    convert_element_type x1 -> x0, local copies, waits for them, and re-layouts: 4.02 us -> none  [per_device(): jnp.transpose(wide_flat.reshape(NX, levels, block_cols), (1, 0, 2))]
    broadcast_in_dim x2 -> x1, local copies, waits for them, and re-layouts: 4.01 us -> 0.04 us  [per_device(): jnp.broadcast_to(jnp.transpose(parts, (1, 0, 2))[:, None, None], (TILES,...]
  transfers between devices with their start and end apart: 3 -> 0, of which waited for: 3 -> 0; matrix products, arithmetic and copies ran while one was open for 0% -> 0% of each run, Pallas kernels for 0% -> 0%
where the time goes in v1:
time: 76.4 us; the launch traced here: 76.1 us
  blocking collectives  65 us (85%)
  Pallas kernels  6.81 us (9%)
  local copies, waits for them, and re-layouts  3.13 us (4%)
    all_to_all x1, blocking collectives, per_device(): lax.all_to_all(sent.reshape(TILES * NEAR, OWN, 2 * ROWS), ('tile', 'near'...  32.5 us
    all_to_all x1, blocking collectives, per_device(): lax.all_to_all(out.reshape(TILES * NEAR, 5, 2, 2 * ROWS), ('tile', 'near'...  22.4 us
    all_to_all x1, blocking collectives, per_device(): gathered = lax.all_to_all(copies, 'far', 0, 0, tiled=True)  10 us
    pallas_call x1, Pallas kernels, per_device(): call(apply_kernel, (shape((LEVELS, ROWS, N), BF16), shape((LEVELS, OWN, M...  2.94 us
    unnamed x17, local copies, waits for them, and re-layouts  2.85 us
    pallas_call x1, Pallas kernels, per_device(): call(nudge_kernel, (shape((TILES, NEAR * OWN, 2 * ROWS), BF16), shape((2,...  1.73 us
    pallas_call x1, Pallas kernels, per_device(): call(project_kernel, shape((TILES, NEAR, OWN, 2 * ROWS), BF16), grid=(NEA...  1.61 us

profile of v1, /device:TPU:1, one launch (start us, length us, event | category | flops | bytes accessed | tf_op | source)
XLA Modules:
  0.0 76.1 jit_solution(7479674726394153256)
XLA Ops:
  0.6 0.0 copy-start
  0.6 1.6 %copy-done = bf16[1,8,64,2048]{3,2,1,0:T(8,128)(2,1)S(1)} copy-done((bf16[1,8,64,2048]{3,2,1,0:T(8,128)(2,1)S(1)}, bf16[1,8,64,2048]{3,2,1,0:T(8,128)(2,1)}, u32[]{:S(2)}) %copy-start) | copy-done | bytes 2097176
  2.2 0.0 copy-start.5
  2.2 1.2 %copy-done.5 = bf16[2048,256]{1,0:T(8,128)(2,1)S(1)} copy-done((bf16[2048,256]{1,0:T(8,128)(2,1)S(1)}, bf16[2048,256]{1,0:T(8,128)(2,1)}, u32[]{:S(2)}) %copy-start.5) | copy-done | bytes 1048600
  3.4 0.0 copy-start.2
  3.5 0.0 copy-start.3
  3.5 1.6 %shard_map.86 = bf16[32,4,8,128]{3,2,1,0:T(8,128)(2,1)S(1)} custom-call(bf16[8,64,2048]{2,1,0:T(8,128)(2,1)S(1)} %bitcast.13, bf16[2048,256]{1,0:T(8,128)(2,1)S(1)} %copy-done.5), custom_call_target="tpu_custom_call" | custom-call | tf_op jit(solution)/shard_map/pallas_call | solution.py:149
  5.1 0.0 copy-start.6
  5.1 0.0 copy-start.7
  5.1 32.5 %all_to_all.15 = bf16[128,8,128]{2,1,0:T(8,128)(2,1)S(1)} all-to-all(bf16[128,8,128]{2,1,0:T(8,128)(2,1)S(1)} %bitcast.17), channel_id=1, replica_groups=mesh['far'=4,'near'=4,'tile'=32] {'tile','near'}, dimensions={0} | all-to-all | bytes 524288 | tf_op jit(solution)/shard_map/all_to_all | solution.py:156
  37.6 0.0 copy-done.2
  37.6 0.0 copy-done.3
  37.6 0.5 shard_map.87
  38.1 10.0 %all_to_all.16.all_ref = f32[4,64,256]{2,1,0:T(8,128)S(1)} all-to-all(f32[4,64,256]{2,1,0:T(8,128)S(1)} %get-tuple-element.8), channel_id=1, replica_groups=mesh['far'=4,'near'=4,'tile'=32] {'far'}, dimensions={0} | all-to-all | bytes 524288 | tf_op jit(solution)/shard_map/all_to_all | solution.py:166
  48.1 0.0 copy-done.6
  48.1 0.0 copy-done.7
  48.1 0.0 copy-start.1
  48.1 0.0 copy-start.4
  48.2 1.7 %shard_map.88 = (bf16[32,32,128]{2,1,0:T(8,128)(2,1)S(1)}, bf16[2,32,128]{2,1,0:T(8,128)(2,1)S(1)}) custom-call(f32[4,64,256]{2,1,0:T(8,128)S(1)} %all_to_all.16.all_ref, f32[64,256]{1,0:T(8,128)S(1)} %get-tuple-element.9.own_ref, f32[8]{0:T(128)S(1)} %copy-done.6, f32[8]{0:T(128)S(1)} %copy-done.7, bf16[2048,256]{1,0:T(8,128)(2,1)S(1)} %copy-done.3, ...), custom_call_target="tpu_custom_call" | custom-call | tf_op jit(solution)/shard_map/pallas_call | solution.py:167
  50.0 0.4 pad_maximum_fusion
  50.4 22.4 %all_to_all.17 = bf16[128,5,2,128]{3,2,1,0:T(2,128)(2,1)S(1)} all-to-all(bf16[128,5,2,128]{3,2,1,0:T(2,128)(2,1)S(1)} %pad_maximum_fusion), channel_id=1, replica_groups=mesh['far'=4,'near'=4,'tile'=32] {'tile','near'}, dimensions={0} | all-to-all | bytes 655360 | tf_op jit(solution)/shard_map/all_to_all | solution.py:177
  72.9 0.2 slice.8
  73.1 0.0 copy-done.1
  73.1 0.0 copy-done.4
  73.1 2.9 %shard_map.89 = (bf16[8,64,2048]{2,1,0:T(8,128)(2,1)}, f32[8,8,256]{2,1,0:T(8,128)}) custom-call(bf16[8,64,2048]{2,1,0:T(8,128)(2,1)S(1)} %bitcast.14, bf16[32,4,8,128]{3,2,1,0:T(8,128)(2,1)S(1)} %bitcast.16, bf16[2,128,128]{2,1,0:T(8,128)(2,1)S(1)} %bitcast.18, bf16[256,2048]{1,0:T(8,128)(2,1)S(1)} %copy-done.4), custom_call_target="tpu_custom_call" | custom-call | tf_op jit(solution)/shard_map/pallas_call | solution.py:182
  (4 shorter events, 0.1 us)
Async XLA Ops:
  0.6 1.6 %copy-start = (bf16[1,8,64,2048]{3,2,1,0:T(8,128)(2,1)S(1)}, bf16[1,8,64,2048]{3,2,1,0:T(8,128)(2,1)}, u32[]{:S(2)}) copy-start(bf16[1,8,64,2048]{3,2,1,0:T(8,128)(2,1)} %param.7) | copy-start | bytes 6291460
  2.2 1.2 %copy-start.5 = (bf16[2048,256]{1,0:T(8,128)(2,1)S(1)}, bf16[2048,256]{1,0:T(8,128)(2,1)}, u32[]{:S(2)}) copy-start(bf16[2048,256]{1,0:T(8,128)(2,1)} %constant.8.clone.by_ref) | copy-start | bytes 3145732
  3.4 34.1 %copy-start.2 = (bf16[2048,256]{1,0:T(8,128)(2,1)S(1)}, bf16[2048,256]{1,0:T(8,128)(2,1)}, u32[]{:S(2)}) copy-start(bf16[2048,256]{1,0:T(8,128)(2,1)} %constant.10.clone.low_ref) | copy-start | bytes 3145732
  3.5 34.1 %copy-start.3 = (bf16[2048,256]{1,0:T(8,128)(2,1)S(1)}, bf16[2048,256]{1,0:T(8,128)(2,1)}, u32[]{:S(2)}) copy-start(bf16[2048,256]{1,0:T(8,128)(2,1)} %constant.9.clone.high_ref) | copy-start | bytes 3145732
  5.1 43.1 %copy-start.6 = (f32[8]{0:T(128)S(1)}, f32[8]{0:T(128)}, u32[]{:S(2)}) copy-start(f32[8]{0:T(128)} %obs_ref.1) | copy-start | bytes 100
  5.1 43.1 %copy-start.7 = (f32[8]{0:T(128)S(1)}, f32[8]{0:T(128)}, u32[]{:S(2)}) copy-start(f32[8]{0:T(128)} %relax_ref.1) | copy-start | bytes 100
  48.1 25.0 %copy-start.1 = (bf16[1,8,64,2048]{3,2,1,0:T(8,128)(2,1)S(1)}, bf16[1,8,64,2048]{3,2,1,0:T(8,128)(2,1)}, u32[]{:S(2)}) copy-start(bf16[1,8,64,2048]{3,2,1,0:T(8,128)(2,1)} %param.7) | copy-start | bytes 6291460
  48.1 25.0 %copy-start.4 = (bf16[256,2048]{1,0:T(8,128)(2,1)S(1)}, bf16[256,2048]{1,0:T(8,128)(2,1)}, u32[]{:S(2)}) copy-start(bf16[256,2048]{1,0:T(8,128)(2,1)} %constant.11.clone.by_ref) | copy-start | bytes 3145732

commit v2 on v1

--- a/solution.py
+++ b/solution.py
@@ -18,6 +18,8 @@
 NEAR = 4
 FAR = MEMBERS // NEAR
 OWN = MODES // TILES
+STEPS = 4
+MIB = 1024 * 1024
 BF16 = jnp.bfloat16
 F32 = jnp.float32
 
@@ -40,17 +42,35 @@
     bx_high = bx.astype(BF16)
     bx_low = (bx - bx_high.astype(np.float32)).astype(BF16)
     by = half[:, second]
-    return bx_high, bx_low, by, np.ascontiguousarray(by.T)
+    flip = lambda a: np.ascontiguousarray(a.T)
+    return bx_high, bx_low, flip(bx_high), flip(bx_low), by, flip(by)
 
 
 def dot(a, b, dims):
     return lax.dot_general(a, b, (dims, ((), ())), preferred_element_type=F32)
 
 
-def project_kernel(states_ref, by_ref, out_ref):
-    field = states_ref[...].reshape(2 * ROWS, N)
-    half = dot(field, by_ref[...], ((1,), (0,)))
-    out_ref[...] = half.T.reshape(TILES, 1, OWN, 2 * ROWS).astype(BF16)
+def project_kernel(states_ref, by_ref, out_ref, field, table, acc, sems):
+    width = N // STEPS
+
+    def copies(k):
+        cols = pl.ds(width * k, width)
+        return (
+            pltpu.make_async_copy(by_ref.at[cols, :], table.at[k], sems.at[2 * k]),
+            pltpu.make_async_copy(states_ref.at[:, :, cols], field.at[k], sems.at[2 * k + 1]),
+        )
+
+    for k in range(STEPS):
+        for c in copies(k):
+            c.start()
+    for k in range(STEPS):
+        for c in copies(k):
+            c.wait()
+        part = dot(field[k].reshape(LEVELS * ROWS, width), table[k], ((1,), (0,)))
+        acc[...] = part if k == 0 else acc[...] + part
+    for c in range(NEAR):
+        half = acc[2 * ROWS * c : 2 * ROWS * (c + 1), :]
+        out_ref[:, c] = half.astype(BF16).T.reshape(TILES, OWN, 2 * ROWS)
 
 
 def coeffs_kernel(rows_ref, high_ref, low_ref, out_ref, copies_ref, wide):
@@ -87,8 +107,10 @@
     misfit = jnp.concatenate(misfits, axis=0)
     high = misfit.astype(BF16)
     low = (misfit - high.astype(F32)).astype(BF16)
-    nt = ((1,), (1,))
-    back = dot(high, high_ref[...], nt) + dot(low, high_ref[...], nt) + dot(high, low_ref[...], nt)
+    nn = ((1,), (0,))
+    count = 2 * NEAR * OWN
+    both = dot(jnp.concatenate([high, low], axis=0), high_ref[...], nn)
+    back = both[:count] + both[count:] + dot(high, low_ref[...], nn)
     back = back.astype(BF16)
     for u in range(TILES // 2):
         a = back[: NEAR * OWN, 2 * ROWS * u : 2 * ROWS * (u + 1)]
@@ -103,32 +125,45 @@
     spread_ref[1] = (flipped - high.astype(F32)).astype(BF16)
 
 
-def apply_kernel(states_ref, back_ref, parts_ref, by_ref, out_ref, spread_ref, mixed, turned):
-    modes = back_ref[...].reshape(MODES, 2 * ROWS)
-    increment = dot(modes, by_ref[...], ((0,), (0,)))
-    field = states_ref[...].reshape(2 * ROWS, N)
-    out_ref[...] = (field.astype(F32) + increment).astype(BF16).reshape(2, ROWS, N)
-
-    @pl.when(pl.program_id(0) == 0)
-    def _():
-        mixed[...] = parts_ref[0].astype(F32) + parts_ref[1].astype(F32)
-        ordered = jnp.concatenate(
-            [mixed[pl.ds(c, TILES, stride=NEAR), :] for c in range(NEAR)], axis=0
-        )
-        turned[...] = ordered.T
-        for l in range(2):
-            strips = [turned[pl.ds(OWN * l + k, OWN, stride=2 * OWN), :] for k in range(OWN)]
-            for c in range(NEAR):
-                spread_ref[2 * c + l] = jnp.concatenate(
-                    [s[:, TILES * c : TILES * (c + 1)] for s in strips], axis=1
-                )
-
-
-def call(kernel, outs, **kw):
+def apply_kernel(
+    states_ref, back_ref, parts_ref, by_ref, out_ref, spread_ref, modes, filled, mixed, turned, sems
+):
+    width = N // STEPS
+    for c in range(NEAR):
+        block = back_ref[:, c].reshape(MODES, 2 * ROWS)
+        modes[2 * ROWS * c : 2 * ROWS * (c + 1), :] = block.T
+
+    def copy(k):
+        cols = pl.ds(width * k, width)
+        return pltpu.make_async_copy(filled.at[k], out_ref.at[:, :, cols], sems.at[k])
+
+    for k in range(STEPS):
+        cols = slice(width * k, width * (k + 1))
+        increment = dot(modes[...], by_ref[:, cols], ((1,), (0,)))
+        field = states_ref[:, :, cols].astype(F32)
+        filled[k] = (field + increment.reshape(LEVELS, ROWS, width)).astype(BF16)
+        copy(k).start()
+
+    mixed[...] = parts_ref[0].astype(F32) + parts_ref[1].astype(F32)
+    ordered = jnp.concatenate(
+        [mixed[pl.ds(c, TILES, stride=NEAR), :] for c in range(NEAR)], axis=0
+    )
+    turned[...] = ordered.T
+    for l in range(2):
+        strips = [turned[pl.ds(OWN * l + k, OWN, stride=2 * OWN), :] for k in range(OWN)]
+        for c in range(NEAR):
+            spread_ref[2 * c + l] = jnp.concatenate(
+                [s[:, TILES * c : TILES * (c + 1)] for s in strips], axis=1
+            )
+    for k in range(STEPS):
+        copy(k).wait()
+
+
+def call(kernel, outs, limit=24 * MIB, **kw):
     return pl.pallas_call(
         kernel,
         out_shape=outs,
-        compiler_params=pltpu.CompilerParams(vmem_limit_bytes=24 * 1024 * 1024),
+        compiler_params=pltpu.CompilerParams(vmem_limit_bytes=limit),
         **kw,
     )
 
@@ -138,20 +173,25 @@
 
 
 def per_device(consts, states, obs_var, relax_rate):
-    bx_high, bx_low, by, by_t = consts
+    bx_high, bx_low, bx_high_t, bx_low_t, by, by_t = consts
     field = states[0]
-    whole = lambda *dims: pl.BlockSpec(dims, lambda i: (0,) * len(dims))
-    levels = pl.BlockSpec((2, ROWS, N), lambda i: (i, 0, 0))
-    chunks = pl.BlockSpec((TILES, 1, OWN, 2 * ROWS), lambda i: (0, i, 0, 0))
+    hbm = pl.BlockSpec(memory_space=pltpu.HBM)
     smem = pl.BlockSpec(memory_space=pltpu.SMEM)
     vmem = pl.BlockSpec(memory_space=pltpu.VMEM)
+    width = N // STEPS
 
     sent = call(
         project_kernel,
         shape((TILES, NEAR, OWN, 2 * ROWS), BF16),
-        grid=(NEAR,),
-        in_specs=[levels, whole(N, MODES)],
-        out_specs=chunks,
+        limit=62 * MIB + MIB // 2,
+        in_specs=[hbm, hbm],
+        out_specs=vmem,
+        scratch_shapes=[
+            pltpu.VMEM((STEPS, LEVELS, ROWS, width), BF16),
+            pltpu.VMEM((STEPS, width, MODES), BF16),
+            pltpu.VMEM((LEVELS * ROWS, MODES), F32),
+            pltpu.SemaphoreType.DMA((2 * STEPS,)),
+        ],
     )(field, by)
     rows = lax.all_to_all(
         sent.reshape(TILES * NEAR, OWN, 2 * ROWS), ("tile", "near"), 0, 0, tiled=True
@@ -169,7 +209,7 @@
         (shape((TILES, NEAR * OWN, 2 * ROWS), BF16), shape((2, TILES, 2 * OWN * OWN), BF16)),
         in_specs=[vmem, vmem, smem, smem, vmem, vmem],
         out_specs=(vmem, vmem),
-    )(gathered, coeffs, obs_var, relax_rate, bx_high, bx_low)
+    )(gathered, coeffs, obs_var, relax_rate, bx_high_t, bx_low_t)
     extra = jnp.broadcast_to(
         jnp.transpose(parts, (1, 0, 2))[:, None, None], (TILES, NEAR, 1, 2, 2 * ROWS)
     )
@@ -182,10 +222,15 @@
     nudged, spread = call(
         apply_kernel,
         (shape((LEVELS, ROWS, N), BF16), shape((LEVELS, OWN, MODES), F32)),
-        grid=(NEAR,),
-        in_specs=[levels, chunks, whole(2, TILES * NEAR, 2 * ROWS), whole(MODES, N)],
-        out_specs=(levels, whole(LEVELS, OWN, MODES)),
-        scratch_shapes=[pltpu.VMEM((2 * ROWS, 2 * ROWS), F32)] * 2,
+        in_specs=[vmem] * 4,
+        out_specs=(hbm, vmem),
+        scratch_shapes=[
+            pltpu.VMEM((LEVELS * ROWS, MODES), BF16),
+            pltpu.VMEM((STEPS, LEVELS, ROWS, width), BF16),
+            pltpu.VMEM((2 * ROWS, 2 * ROWS), F32),
+            pltpu.VMEM((2 * ROWS, 2 * ROWS), F32),
+            pltpu.SemaphoreType.DMA((STEPS,)),
+        ],
     )(field, modes, parts, by_t)
     return nudged[None], spread
 

time: 76.4 us -> 75.8 us (level)
  local copies, waits for them, and re-layouts: 3.13 us -> 1.56 us
    pallas_call x1, Pallas kernels: 1.61 us -> 3.49 us  [per_device(): call(project_kernel, shape((TILES, NEAR, OWN, 2 * ROWS), BF16), limit=62...]
    unnamed x17, local copies, waits for them, and re-layouts: 2.85 us -> 1.28 us
where the time goes in v2:
time: 75.8 us; the launch traced here: 75.6 us
  blocking collectives  65.3 us (86%)
  Pallas kernels  7.49 us (10%)
  local copies, waits for them, and re-layouts  1.56 us (2%)
  between operations  0.78 us (1%)
    all_to_all x1, blocking collectives, per_device(): lax.all_to_all(sent.reshape(TILES * NEAR, OWN, 2 * ROWS), ('tile', 'near'...  32.8 us
    all_to_all x1, blocking collectives, per_device(): lax.all_to_all(out.reshape(TILES * NEAR, 5, 2, 2 * ROWS), ('tile', 'near'...  22.4 us
    all_to_all x1, blocking collectives, per_device(): gathered = lax.all_to_all(copies, 'far', 0, 0, tiled=True)  10 us
    pallas_call x1, Pallas kernels, per_device(): call(project_kernel, shape((TILES, NEAR, OWN, 2 * ROWS), BF16), limit=62...  3.49 us
    pallas_call x1, Pallas kernels, per_device(): call(apply_kernel, (shape((LEVELS, ROWS, N), BF16), shape((LEVELS, OWN, M...  2.31 us

profile of v2, /device:TPU:1, one launch (start us, length us, event | category | flops | bytes accessed | tf_op | source)
XLA Modules:
  0.0 75.6 jit_solution(3012199387612107724)
XLA Ops:
  0.6 0.0 copy-start.4
  0.6 0.0 copy-start.6
  0.7 0.0 copy-start.7
  0.7 3.5 %shard_map.104 = bf16[32,4,8,128]{3,2,1,0:T(8,128)(2,1)} custom-call(bf16[8,64,2048]{2,1,0:T(8,128)(2,1)} %bitcast.13, bf16[2048,256]{1,0:T(8,128)(2,1)} %constant.12.clone.by_ref), custom_call_target="tpu_custom_call" | custom-call | tf_op jit(solution)/shard_map/pallas_call | solution.py:183
  4.2 0.0 copy-start.2
  4.2 0.0 copy-start.3
  4.2 32.8 %all_to_all.15 = bf16[128,8,128]{2,1,0:T(8,128)(2,1)S(1)} all-to-all(bf16[128,8,128]{2,1,0:T(8,128)(2,1)} %bitcast.20), channel_id=1, replica_groups=mesh['far'=4,'near'=4,'tile'=32] {'tile','near'}, dimensions={0} | all-to-all | bytes 524288 | tf_op jit(solution)/shard_map/all_to_all | solution.py:196
  37.0 0.0 copy-done.4
  37.0 0.0 copy-start.5
  37.0 1.2 %copy-done.5 = bf16[2048,256]{1,0:T(8,128)(2,1)S(1)} copy-done((bf16[2048,256]{1,0:T(8,128)(2,1)S(1)}, bf16[2048,256]{1,0:T(8,128)(2,1)}, u32[]{:S(2)}) %copy-start.5) | copy-done | bytes 1048600
  38.2 0.5 shard_map.105
  38.8 10.0 %all_to_all.16.all_ref = f32[4,64,256]{2,1,0:T(8,128)S(1)} all-to-all(f32[4,64,256]{2,1,0:T(8,128)S(1)} %get-tuple-element.8), channel_id=1, replica_groups=mesh['far'=4,'near'=4,'tile'=32] {'far'}, dimensions={0} | all-to-all | bytes 524288 | tf_op jit(solution)/shard_map/all_to_all | solution.py:206
  48.8 0.0 copy-done.6
  48.8 0.0 copy-done.7
  48.8 0.0 copy-done.2
  48.8 0.0 copy-done.3
  48.8 0.0 copy-start
  48.8 0.0 copy-start.1
  48.8 1.2 %shard_map.106 = (bf16[32,32,128]{2,1,0:T(8,128)(2,1)S(1)}, bf16[2,32,128]{2,1,0:T(8,128)(2,1)S(1)}) custom-call(f32[4,64,256]{2,1,0:T(8,128)S(1)} %all_to_all.16.all_ref, f32[64,256]{1,0:T(8,128)S(1)} %get-tuple-element.9.own_ref, f32[8]{0:T(128)S(1)} %copy-done.6, f32[8]{0:T(128)S(1)} %copy-done.7, bf16[256,2048]{1,0:T(8,128)(2,1)S(1)} %copy-done.3, ...), custom_call_target="tpu_custom_call" | custom-call | tf_op jit(solution)/shard_map/pallas_call | solution.py:207
  50.1 0.4 pad_maximum_fusion
  50.5 22.4 %all_to_all.17 = bf16[128,5,2,128]{3,2,1,0:T(2,128)(2,1)S(1)} all-to-all(bf16[128,5,2,128]{3,2,1,0:T(2,128)(2,1)S(1)} %pad_maximum_fusion), channel_id=1, replica_groups=mesh['far'=4,'near'=4,'tile'=32] {'tile','near'}, dimensions={0} | all-to-all | bytes 655360 | tf_op jit(solution)/shard_map/all_to_all | solution.py:217
  73.0 0.2 slice.8
  73.2 0.0 copy-done
  73.2 0.0 copy-done.1
  73.3 2.3 %shard_map.107 = (bf16[8,64,2048]{2,1,0:T(8,128)(2,1)}, f32[8,8,256]{2,1,0:T(8,128)}) custom-call(bf16[8,64,2048]{2,1,0:T(8,128)(2,1)S(1)} %bitcast.14, bf16[32,4,8,128]{3,2,1,0:T(8,128)(2,1)S(1)} %bitcast.16, bf16[2,128,128]{2,1,0:T(8,128)(2,1)S(1)} %bitcast.17, bf16[256,2048]{1,0:T(8,128)(2,1)S(1)} %copy-done.1), custom_call_target="tpu_custom_call" | custom-call | tf_op jit(solution)/shard_map/pallas_call | solution.py:222
  (4 shorter events, 0.1 us)
Async XLA Ops:
  0.6 36.4 %copy-start.4 = (bf16[2048,256]{1,0:T(8,128)(2,1)S(1)}, bf16[2048,256]{1,0:T(8,128)(2,1)}, u32[]{:S(2)}) copy-start(bf16[2048,256]{1,0:T(8,128)(2,1)} %constant.14.clone.low_ref) | copy-start | bytes 3145732
  0.6 48.2 %copy-start.6 = (f32[8]{0:T(128)S(1)}, f32[8]{0:T(128)}, u32[]{:S(2)}) copy-start(f32[8]{0:T(128)} %obs_ref.1) | copy-start | bytes 100
  0.7 48.2 %copy-start.7 = (f32[8]{0:T(128)S(1)}, f32[8]{0:T(128)}, u32[]{:S(2)}) copy-start(f32[8]{0:T(128)} %relax_ref.1) | copy-start | bytes 100
  4.2 44.6 %copy-start.2 = (bf16[256,2048]{1,0:T(8,128)(2,1)S(1)}, bf16[256,2048]{1,0:T(8,128)(2,1)}, u32[]{:S(2)}) copy-start(bf16[256,2048]{1,0:T(8,128)(2,1)} %constant.16.clone.low_ref) | copy-start | bytes 3145732
  4.2 44.6 %copy-start.3 = (bf16[256,2048]{1,0:T(8,128)(2,1)S(1)}, bf16[256,2048]{1,0:T(8,128)(2,1)}, u32[]{:S(2)}) copy-start(bf16[256,2048]{1,0:T(8,128)(2,1)} %constant.15.clone.high_ref) | copy-start | bytes 3145732
  37.0 1.2 %copy-start.5 = (bf16[2048,256]{1,0:T(8,128)(2,1)S(1)}, bf16[2048,256]{1,0:T(8,128)(2,1)}, u32[]{:S(2)}) copy-start(bf16[2048,256]{1,0:T(8,128)(2,1)} %constant.13.clone.high_ref) | copy-start | bytes 3145732
  48.8 24.4 %copy-start = (bf16[1,8,64,2048]{3,2,1,0:T(8,128)(2,1)S(1)}, bf16[1,8,64,2048]{3,2,1,0:T(8,128)(2,1)}, u32[]{:S(2)}) copy-start(bf16[1,8,64,2048]{3,2,1,0:T(8,128)(2,1)} %param.9) | copy-start | bytes 6291460
  48.8 24.4 %copy-start.1 = (bf16[256,2048]{1,0:T(8,128)(2,1)S(1)}, bf16[256,2048]{1,0:T(8,128)(2,1)}, u32[]{:S(2)}) copy-start(bf16[256,2048]{1,0:T(8,128)(2,1)} %constant.17.clone.by_ref) | copy-start | bytes 3145732

commit v3 on v2

--- a/solution.py
+++ b/solution.py
@@ -19,6 +19,7 @@
 FAR = MEMBERS // NEAR
 OWN = MODES // TILES
 STEPS = 4
+CHUNK = OWN + 2
 MIB = 1024 * 1024
 BF16 = jnp.bfloat16
 F32 = jnp.float32
@@ -86,7 +87,7 @@
         copies_ref[k] = coeffs
 
 
-def nudge_kernel(all_ref, own_ref, obs_ref, relax_ref, high_ref, low_ref, rows_ref, spread_ref):
+def nudge_kernel(all_ref, own_ref, obs_ref, relax_ref, high_ref, low_ref, sent_ref):
     pair = lax.axis_index("near")
     spreads, misfits = [], []
     for l in range(2):
@@ -111,27 +112,36 @@
     count = 2 * NEAR * OWN
     both = dot(jnp.concatenate([high, low], axis=0), high_ref[...], nn)
     back = both[:count] + both[count:] + dot(high, low_ref[...], nn)
-    back = back.astype(BF16)
-    for u in range(TILES // 2):
-        a = back[: NEAR * OWN, 2 * ROWS * u : 2 * ROWS * (u + 1)]
-        b = back[NEAR * OWN :, 2 * ROWS * u : 2 * ROWS * (u + 1)]
-        rows_ref[2 * u] = jnp.concatenate([a[:, :ROWS], b[:, :ROWS]], axis=1)
-        rows_ref[2 * u + 1] = jnp.concatenate([a[:, ROWS:], b[:, ROWS:]], axis=1)
-    both = jnp.concatenate(spreads, axis=0)
-    stacked = jnp.concatenate([both[:, TILES * k : TILES * (k + 1)] for k in range(OWN)], axis=0)
-    flipped = stacked.T
-    high = flipped.astype(BF16)
-    spread_ref[0] = high
-    spread_ref[1] = (flipped - high.astype(F32)).astype(BF16)
+    stacked = jnp.concatenate(spreads, axis=0)
+    stacked = jnp.concatenate(
+        [stacked[:, TILES * k : TILES * (k + 1)] for k in range(OWN)], axis=0
+    ).T
+    first = stacked.astype(BF16).astype(F32)
+    second = stacked - first
+    for t in range(TILES):
+        half = slice(ROWS * t, ROWS * (t + 1))
+        rows = jnp.concatenate([back[: NEAR * OWN, half], back[NEAR * OWN :, half]], axis=1)
+        extra = jnp.concatenate([first[t : t + 1], second[t : t + 1]], axis=0)
+        pieces = []
+        for k in range(NEAR):
+            pieces += [rows[OWN * k : OWN * (k + 1)], extra]
+        sent_ref[NEAR * CHUNK * t : NEAR * CHUNK * (t + 1), :] = jnp.concatenate(
+            pieces, axis=0
+        ).astype(BF16)
 
 
 def apply_kernel(
-    states_ref, back_ref, parts_ref, by_ref, out_ref, spread_ref, modes, filled, mixed, turned, sems
+    states_ref, got_ref, by_ref, out_ref, spread_ref, back, modes, filled, mixed, turned, sems
 ):
     width = N // STEPS
+    for t in range(TILES):
+        rows = got_ref[NEAR * CHUNK * t : NEAR * CHUNK * (t + 1), :].astype(F32)
+        for c in range(NEAR):
+            piece = rows[CHUNK * c : CHUNK * (c + 1)]
+            back[c, OWN * t : OWN * (t + 1), :] = piece[:OWN]
+            mixed[TILES * c + t : TILES * c + t + 1, :] = piece[OWN : OWN + 1] + piece[OWN + 1 :]
     for c in range(NEAR):
-        block = back_ref[:, c].reshape(MODES, 2 * ROWS)
-        modes[2 * ROWS * c : 2 * ROWS * (c + 1), :] = block.T
+        modes[2 * ROWS * c : 2 * ROWS * (c + 1), :] = back[c].astype(BF16).T
 
     def copy(k):
         cols = pl.ds(width * k, width)
@@ -144,11 +154,7 @@
         filled[k] = (field + increment.reshape(LEVELS, ROWS, width)).astype(BF16)
         copy(k).start()
 
-    mixed[...] = parts_ref[0].astype(F32) + parts_ref[1].astype(F32)
-    ordered = jnp.concatenate(
-        [mixed[pl.ds(c, TILES, stride=NEAR), :] for c in range(NEAR)], axis=0
-    )
-    turned[...] = ordered.T
+    turned[...] = mixed[...].T
     for l in range(2):
         strips = [turned[pl.ds(OWN * l + k, OWN, stride=2 * OWN), :] for k in range(OWN)]
         for c in range(NEAR):
@@ -183,7 +189,6 @@
     sent = call(
         project_kernel,
         shape((TILES, NEAR, OWN, 2 * ROWS), BF16),
-        limit=62 * MIB + MIB // 2,
         in_specs=[hbm, hbm],
         out_specs=vmem,
         scratch_shapes=[
@@ -192,7 +197,7 @@
             pltpu.VMEM((LEVELS * ROWS, MODES), F32),
             pltpu.SemaphoreType.DMA((2 * STEPS,)),
         ],
-    )(field, by)
+    )(*(pltpu.with_memory_space_constraint(x, pltpu.HBM) for x in (field, by)))
     rows = lax.all_to_all(
         sent.reshape(TILES * NEAR, OWN, 2 * ROWS), ("tile", "near"), 0, 0, tiled=True
     )
@@ -204,34 +209,29 @@
         scratch_shapes=[pltpu.VMEM((2 * NEAR * OWN, N), BF16)],
     )(rows.reshape(TILES, NEAR * OWN, 2 * ROWS), bx_high, bx_low)
     gathered = lax.all_to_all(copies, "far", 0, 0, tiled=True)
-    back, parts = call(
+    sent = call(
         nudge_kernel,
-        (shape((TILES, NEAR * OWN, 2 * ROWS), BF16), shape((2, TILES, 2 * OWN * OWN), BF16)),
+        shape((TILES * NEAR * CHUNK, 2 * ROWS), BF16),
         in_specs=[vmem, vmem, smem, smem, vmem, vmem],
-        out_specs=(vmem, vmem),
+        out_specs=vmem,
     )(gathered, coeffs, obs_var, relax_rate, bx_high_t, bx_low_t)
-    extra = jnp.broadcast_to(
-        jnp.transpose(parts, (1, 0, 2))[:, None, None], (TILES, NEAR, 1, 2, 2 * ROWS)
-    )
-    out = jnp.concatenate([back.reshape(TILES, NEAR, 4, 2, 2 * ROWS), extra], axis=2)
     got = lax.all_to_all(
-        out.reshape(TILES * NEAR, 5, 2, 2 * ROWS), ("tile", "near"), 0, 0, tiled=True
-    )
-    modes = got[:, :4].reshape(TILES, NEAR, OWN, 2 * ROWS)
-    parts = jnp.transpose(got[:, 4], (1, 0, 2))
+        sent.reshape(TILES * NEAR, CHUNK // 2, 2, 2 * ROWS), ("tile", "near"), 0, 0, tiled=True
+    )
     nudged, spread = call(
         apply_kernel,
         (shape((LEVELS, ROWS, N), BF16), shape((LEVELS, OWN, MODES), F32)),
-        in_specs=[vmem] * 4,
+        in_specs=[vmem] * 3,
         out_specs=(hbm, vmem),
         scratch_shapes=[
+            pltpu.VMEM((NEAR, MODES, 2 * ROWS), F32),
             pltpu.VMEM((LEVELS * ROWS, MODES), BF16),
             pltpu.VMEM((STEPS, LEVELS, ROWS, width), BF16),
             pltpu.VMEM((2 * ROWS, 2 * ROWS), F32),
             pltpu.VMEM((2 * ROWS, 2 * ROWS), F32),
             pltpu.SemaphoreType.DMA((STEPS,)),
         ],
-    )(field, modes, parts, by_t)
+    )(field, got.reshape(TILES * NEAR * CHUNK, 2 * ROWS), by_t)
     return nudged[None], spread
 
 

time: 75.8 us -> 73.2 us (0.966)
  local copies, waits for them, and re-layouts: 1.56 us -> 0.05 us
    unnamed x17 -> x16, local copies, waits for them, and re-layouts: 1.28 us -> 0.05 us
where the time goes in v3:
time: 73.2 us; the launch traced here: 73 us
  blocking collectives  65.3 us (89%)
  Pallas kernels  6.92 us (9%)
    all_to_all x1, blocking collectives, per_device(): lax.all_to_all(sent.reshape(TILES * NEAR, OWN, 2 * ROWS), ('tile', 'near'...  32.6 us
    all_to_all x1, blocking collectives, per_device(): lax.all_to_all(sent.reshape(TILES * NEAR, CHUNK // 2, 2, 2 * ROWS), ('til...  22.4 us
    all_to_all x1, blocking collectives, per_device(): gathered = lax.all_to_all(copies, 'far', 0, 0, tiled=True)  10.3 us
    pallas_call x1, Pallas kernels, per_device(): call(project_kernel, shape((TILES, NEAR, OWN, 2 * ROWS), BF16), in_specs=...  2.85 us
    pallas_call x1, Pallas kernels, per_device(): call(apply_kernel, (shape((LEVELS, ROWS, N), BF16), shape((LEVELS, OWN, M...  2.37 us

profile of v3, /device:TPU:1, one launch (start us, length us, event | category | flops | bytes accessed | tf_op | source)
XLA Modules:
  0.0 73.0 jit_solution(15359487566122156052)
XLA Ops:
  0.6 0.0 copy-start.4
  0.6 0.0 copy-start.5
  0.7 2.8 %shard_map.104 = bf16[32,4,8,128]{3,2,1,0:T(8,128)(2,1)S(1)} custom-call(bf16[8,64,2048]{2,1,0:T(8,128)(2,1)} %bitcast.6, bf16[2048,256]{1,0:T(8,128)(2,1)} %constant.12.clone.by_ref), custom_call_target="tpu_custom_call" | custom-call | tf_op jit(solution)/shard_map/pallas_call | solution.py:189
  3.5 0.0 copy-start.1
  3.5 0.0 copy-start.2
  3.5 0.0 copy-start.6
  3.5 0.0 copy-start.7
  3.6 32.6 %all_to_all.15 = bf16[128,8,128]{2,1,0:T(8,128)(2,1)S(1)} all-to-all(bf16[128,8,128]{2,1,0:T(8,128)(2,1)S(1)} %bitcast.11), channel_id=1, replica_groups=mesh['far'=4,'near'=4,'tile'=32] {'tile','near'}, dimensions={0} | all-to-all | bytes 524288 | tf_op jit(solution)/shard_map/all_to_all | solution.py:201
  36.2 0.0 copy-done.4
  36.2 0.0 copy-done.5
  36.2 0.5 shard_map.105
  36.7 0.0 copy-start
  36.7 0.0 copy-start.3
  36.7 10.3 %all_to_all.16.all_ref = f32[4,64,256]{2,1,0:T(8,128)S(1)} all-to-all(f32[4,64,256]{2,1,0:T(8,128)S(1)} %get-tuple-element.6), channel_id=1, replica_groups=mesh['far'=4,'near'=4,'tile'=32] {'far'}, dimensions={0} | all-to-all | bytes 524288 | tf_op jit(solution)/shard_map/all_to_all | solution.py:211
  47.0 0.0 copy-done.1
  47.0 0.0 copy-done.2
  47.0 0.0 copy-done.6
  47.0 0.0 copy-done.7
  47.1 1.2 %shard_map.106 = bf16[1280,128]{1,0:T(8,128)(2,1)S(1)} custom-call(f32[4,64,256]{2,1,0:T(8,128)S(1)} %all_to_all.16.all_ref, f32[64,256]{1,0:T(8,128)S(1)} %get-tuple-element.7.own_ref, f32[8]{0:T(128)S(1)} %copy-done.6, f32[8]{0:T(128)S(1)} %copy-done.7, bf16[256,2048]{1,0:T(8,128)(2,1)S(1)} %copy-done.2, bf16[256,2048]{1,0:T(8,128)(2,1)S(1)} %copy-done.1), custom_call_target="tpu_custom_call" | custom-call | tf_op jit(solution)/shard_map/pallas_call | solution.py:212
  48.2 22.4 %all_to_all.17 = bf16[128,5,2,128]{3,2,1,0:T(2,128)(2,1)S(1)} all-to-all(bf16[128,5,2,128]{3,2,1,0:T(2,128)(2,1)S(1)} %bitcast.8), channel_id=1, replica_groups=mesh['far'=4,'near'=4,'tile'=32] {'tile','near'}, dimensions={0} | all-to-all | bytes 655360 | tf_op jit(solution)/shard_map/all_to_all | solution.py:218
  70.7 0.0 copy-done
  70.7 0.0 copy-done.3
  70.7 2.4 %shard_map.107 = (bf16[8,64,2048]{2,1,0:T(8,128)(2,1)}, f32[8,8,256]{2,1,0:T(8,128)}) custom-call(bf16[8,64,2048]{2,1,0:T(8,128)(2,1)S(1)} %bitcast.7, bf16[1280,128]{1,0:T(8,128)(2,1)S(1)} %bitcast.9, bf16[256,2048]{1,0:T(8,128)(2,1)S(1)} %copy-done.3), custom_call_target="tpu_custom_call" | custom-call | tf_op jit(solution)/shard_map/pallas_call | solution.py:221
Async XLA Ops:
  0.6 35.5 %copy-start.4 = (bf16[2048,256]{1,0:T(8,128)(2,1)S(1)}, bf16[2048,256]{1,0:T(8,128)(2,1)}, u32[]{:S(2)}) copy-start(bf16[2048,256]{1,0:T(8,128)(2,1)} %constant.14.clone.low_ref) | copy-start | bytes 3145732
  0.6 35.5 %copy-start.5 = (bf16[2048,256]{1,0:T(8,128)(2,1)S(1)}, bf16[2048,256]{1,0:T(8,128)(2,1)}, u32[]{:S(2)}) copy-start(bf16[2048,256]{1,0:T(8,128)(2,1)} %constant.13.clone.high_ref) | copy-start | bytes 3145732
  3.5 43.5 %copy-start.1 = (bf16[256,2048]{1,0:T(8,128)(2,1)S(1)}, bf16[256,2048]{1,0:T(8,128)(2,1)}, u32[]{:S(2)}) copy-start(bf16[256,2048]{1,0:T(8,128)(2,1)} %constant.16.clone.low_ref) | copy-start | bytes 3145732
  3.5 43.5 %copy-start.2 = (bf16[256,2048]{1,0:T(8,128)(2,1)S(1)}, bf16[256,2048]{1,0:T(8,128)(2,1)}, u32[]{:S(2)}) copy-start(bf16[256,2048]{1,0:T(8,128)(2,1)} %constant.15.clone.high_ref) | copy-start | bytes 3145732
  3.5 43.5 %copy-start.6 = (f32[8]{0:T(128)S(1)}, f32[8]{0:T(128)}, u32[]{:S(2)}) copy-start(f32[8]{0:T(128)} %obs_ref.1) | copy-start | bytes 100
  3.5 43.5 %copy-start.7 = (f32[8]{0:T(128)S(1)}, f32[8]{0:T(128)}, u32[]{:S(2)}) copy-start(f32[8]{0:T(128)} %relax_ref.1) | copy-start | bytes 100
  36.7 34.0 %copy-start = (bf16[1,8,64,2048]{3,2,1,0:T(8,128)(2,1)S(1)}, bf16[1,8,64,2048]{3,2,1,0:T(8,128)(2,1)}, u32[]{:S(2)}) copy-start(bf16[1,8,64,2048]{3,2,1,0:T(8,128)(2,1)} %param.9) | copy-start | bytes 6291460
  36.7 33.9 %copy-start.3 = (bf16[256,2048]{1,0:T(8,128)(2,1)S(1)}, bf16[256,2048]{1,0:T(8,128)(2,1)}, u32[]{:S(2)}) copy-start(bf16[256,2048]{1,0:T(8,128)(2,1)} %constant.17.clone.by_ref) | copy-start | bytes 3145732

commit v4 on v3

--- a/solution.py
+++ b/solution.py
@@ -19,6 +19,8 @@
 FAR = MEMBERS // NEAR
 OWN = MODES // TILES
 STEPS = 4
+HALF = N // 2
+WIDTH = HALF // STEPS
 CHUNK = OWN + 2
 MIB = 1024 * 1024
 BF16 = jnp.bfloat16
@@ -35,16 +37,20 @@
 
 
 def tables():
-    full = mode_table()
-    half = full.astype(BF16)
+    full = mode_table()[:HALF]
+    high = full.astype(BF16)
+    low = (full - high.astype(np.float32)).astype(BF16)
     first = np.arange(MODES).reshape(TILES, OWN).T.reshape(-1)
     second = np.arange(MODES).reshape(OWN, TILES).T.reshape(-1)
-    bx = full[:, first]
-    bx_high = bx.astype(BF16)
-    bx_low = (bx - bx_high.astype(np.float32)).astype(BF16)
-    by = half[:, second]
     flip = lambda a: np.ascontiguousarray(a.T)
+    bx_high, bx_low, by = high[:, first], low[:, first], high[:, second]
     return bx_high, bx_low, flip(bx_high), flip(bx_low), by, flip(by)
+
+
+def signs(major, minor):
+    column = lax.broadcasted_iota(jnp.int32, (1, MODES), 1)
+    mode = major * (column % minor) + column // minor
+    return (1 - 2 * ((mode + 1) // 2 % 2)).astype(F32)
 
 
 def dot(a, b, dims):
@@ -52,14 +58,14 @@
 
 
 def project_kernel(states_ref, by_ref, out_ref, field, table, acc, sems):
-    width = N // STEPS
-
     def copies(k):
-        cols = pl.ds(width * k, width)
-        return (
-            pltpu.make_async_copy(by_ref.at[cols, :], table.at[k], sems.at[2 * k]),
-            pltpu.make_async_copy(states_ref.at[:, :, cols], field.at[k], sems.at[2 * k + 1]),
-        )
+        rows = pl.ds(WIDTH * k, WIDTH)
+        yield pltpu.make_async_copy(by_ref.at[rows, :], table.at[k], sems.at[3 * k])
+        for h in range(2):
+            cols = pl.ds(HALF * h + WIDTH * k, WIDTH)
+            yield pltpu.make_async_copy(
+                states_ref.at[:, :, cols], field.at[k, h], sems.at[3 * k + 1 + h]
+            )
 
     for k in range(STEPS):
         for c in copies(k):
@@ -67,21 +73,31 @@
     for k in range(STEPS):
         for c in copies(k):
             c.wait()
-        part = dot(field[k].reshape(LEVELS * ROWS, width), table[k], ((1,), (0,)))
-        acc[...] = part if k == 0 else acc[...] + part
+        for h in range(2):
+            part = dot(field[k, h].reshape(LEVELS * ROWS, WIDTH), table[k], ((1,), (0,)))
+            rows = slice(LEVELS * ROWS * h, LEVELS * ROWS * (h + 1))
+            acc[rows, :] = part if k == 0 else acc[rows, :] + part
+    sign = signs(TILES, OWN)
     for c in range(NEAR):
-        half = acc[2 * ROWS * c : 2 * ROWS * (c + 1), :]
-        out_ref[:, c] = half.astype(BF16).T.reshape(TILES, OWN, 2 * ROWS)
+        lower = acc[2 * ROWS * c : 2 * ROWS * (c + 1), :]
+        upper = acc[LEVELS * ROWS + 2 * ROWS * c : LEVELS * ROWS + 2 * ROWS * (c + 1), :]
+        half = (lower + sign * upper).astype(BF16)
+        out_ref[:, c] = half.T.reshape(TILES, OWN, 2 * ROWS)
 
 
 def coeffs_kernel(rows_ref, high_ref, low_ref, out_ref, copies_ref, wide):
+    count = NEAR * OWN
     for u in range(TILES // 2):
         a, b = rows_ref[2 * u], rows_ref[2 * u + 1]
-        cols = pl.ds(2 * ROWS * u, 2 * ROWS)
-        wide[: NEAR * OWN, cols] = jnp.concatenate([a[:, :ROWS], b[:, :ROWS]], axis=1)
-        wide[NEAR * OWN :, cols] = jnp.concatenate([a[:, ROWS:], b[:, ROWS:]], axis=1)
+        row = 2 * count * (u // (TILES // 4))
+        cols = pl.ds(2 * ROWS * (u % (TILES // 4)), 2 * ROWS)
+        wide[row : row + count, cols] = jnp.concatenate([a[:, :ROWS], b[:, :ROWS]], axis=1)
+        wide[row + count : row + 2 * count, cols] = jnp.concatenate(
+            [a[:, ROWS:], b[:, ROWS:]], axis=1
+        )
     x = wide[...]
-    coeffs = dot(x, high_ref[...], ((1,), (0,))) + dot(x, low_ref[...], ((1,), (0,)))
+    both = dot(x, high_ref[...], ((1,), (0,))) + dot(x, low_ref[...], ((1,), (0,)))
+    coeffs = both[: 2 * count] + signs(OWN, TILES) * both[2 * count :]
     out_ref[...] = coeffs
     for k in range(FAR):
         copies_ref[k] = coeffs
@@ -110,8 +126,11 @@
     low = (misfit - high.astype(F32)).astype(BF16)
     nn = ((1,), (0,))
     count = 2 * NEAR * OWN
+    sign = signs(OWN, TILES).astype(BF16)
+    high = jnp.concatenate([high, high * sign], axis=0)
+    low = jnp.concatenate([low, low * sign], axis=0)
     both = dot(jnp.concatenate([high, low], axis=0), high_ref[...], nn)
-    back = both[:count] + both[count:] + dot(high, low_ref[...], nn)
+    back = both[: 2 * count] + both[2 * count :] + dot(high, low_ref[...], nn)
     stacked = jnp.concatenate(spreads, axis=0)
     stacked = jnp.concatenate(
         [stacked[:, TILES * k : TILES * (k + 1)] for k in range(OWN)], axis=0
@@ -119,8 +138,9 @@
     first = stacked.astype(BF16).astype(F32)
     second = stacked - first
     for t in range(TILES):
-        half = slice(ROWS * t, ROWS * (t + 1))
-        rows = jnp.concatenate([back[: NEAR * OWN, half], back[NEAR * OWN :, half]], axis=1)
+        row, col = divmod(t, TILES // 2)
+        block = back[count * row : count * (row + 1), ROWS * col : ROWS * (col + 1)]
+        rows = jnp.concatenate([block[: NEAR * OWN], block[NEAR * OWN :]], axis=1)
         extra = jnp.concatenate([first[t : t + 1], second[t : t + 1]], axis=0)
         pieces = []
         for k in range(NEAR):
@@ -131,29 +151,27 @@
 
 
 def apply_kernel(
-    states_ref, got_ref, by_ref, out_ref, spread_ref, back, modes, filled, mixed, turned, sems
+    states_ref, got_ref, by_ref, out_ref, spread_ref, back, filled, mixed, turned, sems
 ):
-    width = N // STEPS
-    for t in range(TILES):
-        rows = got_ref[NEAR * CHUNK * t : NEAR * CHUNK * (t + 1), :].astype(F32)
-        for c in range(NEAR):
-            piece = rows[CHUNK * c : CHUNK * (c + 1)]
-            back[c, OWN * t : OWN * (t + 1), :] = piece[:OWN]
+    def copy(c):
+        levels = pl.ds(2 * c, 2)
+        return pltpu.make_async_copy(filled.at[levels], out_ref.at[levels], sems.at[c])
+
+    sign = signs(TILES, OWN).astype(BF16)
+    for c in range(NEAR):
+        for t in range(TILES):
+            row = CHUNK * (NEAR * t + c)
+            piece = got_ref[row : row + CHUNK, :].astype(F32)
+            back[OWN * t : OWN * (t + 1), :] = piece[:OWN]
             mixed[TILES * c + t : TILES * c + t + 1, :] = piece[OWN : OWN + 1] + piece[OWN + 1 :]
-    for c in range(NEAR):
-        modes[2 * ROWS * c : 2 * ROWS * (c + 1), :] = back[c].astype(BF16).T
-
-    def copy(k):
-        cols = pl.ds(width * k, width)
-        return pltpu.make_async_copy(filled.at[k], out_ref.at[:, :, cols], sems.at[k])
-
-    for k in range(STEPS):
-        cols = slice(width * k, width * (k + 1))
-        increment = dot(modes[...], by_ref[:, cols], ((1,), (0,)))
-        field = states_ref[:, :, cols].astype(F32)
-        filled[k] = (field + increment.reshape(LEVELS, ROWS, width)).astype(BF16)
-        copy(k).start()
-
+        modes = back[...].astype(BF16).T
+        for h in range(2):
+            cols = slice(HALF * h, HALF * (h + 1))
+            increment = dot(modes if h == 0 else modes * sign, by_ref[...], ((1,), (0,)))
+            field = states_ref[2 * c : 2 * c + 2, :, cols].astype(F32)
+            total = field + increment.reshape(2, ROWS, HALF)
+            filled[2 * c : 2 * c + 2, :, cols] = total.astype(BF16)
+        copy(c).start()
     turned[...] = mixed[...].T
     for l in range(2):
         strips = [turned[pl.ds(OWN * l + k, OWN, stride=2 * OWN), :] for k in range(OWN)]
@@ -161,8 +179,8 @@
             spread_ref[2 * c + l] = jnp.concatenate(
                 [s[:, TILES * c : TILES * (c + 1)] for s in strips], axis=1
             )
-    for k in range(STEPS):
-        copy(k).wait()
+    for c in range(NEAR):
+        copy(c).wait()
 
 
 def call(kernel, outs, limit=24 * MIB, **kw):
@@ -184,7 +202,6 @@
     hbm = pl.BlockSpec(memory_space=pltpu.HBM)
     smem = pl.BlockSpec(memory_space=pltpu.SMEM)
     vmem = pl.BlockSpec(memory_space=pltpu.VMEM)
-    width = N // STEPS
 
     sent = call(
         project_kernel,
@@ -192,10 +209,10 @@
         in_specs=[hbm, hbm],
         out_specs=vmem,
         scratch_shapes=[
-            pltpu.VMEM((STEPS, LEVELS, ROWS, width), BF16),
-            pltpu.VMEM((STEPS, width, MODES), BF16),
-            pltpu.VMEM((LEVELS * ROWS, MODES), F32),
-            pltpu.SemaphoreType.DMA((2 * STEPS,)),
+            pltpu.VMEM((STEPS, 2, LEVELS, ROWS, WIDTH), BF16),
+            pltpu.VMEM((STEPS, WIDTH, MODES), BF16),
+            pltpu.VMEM((2 * LEVELS * ROWS, MODES), F32),
+            pltpu.SemaphoreType.DMA((3 * STEPS,)),
         ],
     )(*(pltpu.with_memory_space_constraint(x, pltpu.HBM) for x in (field, by)))
     rows = lax.all_to_all(
@@ -206,7 +223,7 @@
         (shape((2 * NEAR * OWN, MODES), F32), shape((FAR, 2 * NEAR * OWN, MODES), F32)),
         in_specs=[vmem] * 3,
         out_specs=(vmem, vmem),
-        scratch_shapes=[pltpu.VMEM((2 * NEAR * OWN, N), BF16)],
+        scratch_shapes=[pltpu.VMEM((4 * NEAR * OWN, HALF), BF16)],
     )(rows.reshape(TILES, NEAR * OWN, 2 * ROWS), bx_high, bx_low)
     gathered = lax.all_to_all(copies, "far", 0, 0, tiled=True)
     sent = call(
@@ -224,12 +241,11 @@
         in_specs=[vmem] * 3,
         out_specs=(hbm, vmem),
         scratch_shapes=[
-            pltpu.VMEM((NEAR, MODES, 2 * ROWS), F32),
-            pltpu.VMEM((LEVELS * ROWS, MODES), BF16),
-            pltpu.VMEM((STEPS, LEVELS, ROWS, width), BF16),
+            pltpu.VMEM((MODES, 2 * ROWS), F32),
+            pltpu.VMEM((LEVELS, ROWS, N), BF16),
             pltpu.VMEM((2 * ROWS, 2 * ROWS), F32),
             pltpu.VMEM((2 * ROWS, 2 * ROWS), F32),
-            pltpu.SemaphoreType.DMA((STEPS,)),
+            pltpu.SemaphoreType.DMA((NEAR,)),
         ],
     )(field, got.reshape(TILES * NEAR * CHUNK, 2 * ROWS), by_t)
     return nudged[None], spread

time: 73.2 us -> 72.3 us (0.988)
  no operation moved by 1% of the time
where the time goes in v4:
time: 72.3 us; the launch traced here: 72.1 us
  blocking collectives  65.1 us (90%)
  Pallas kernels  6.21 us (9%)
    all_to_all x1, blocking collectives, per_device(): lax.all_to_all(sent.reshape(TILES * NEAR, OWN, 2 * ROWS), ('tile', 'near'...  32.5 us
    all_to_all x1, blocking collectives, per_device(): lax.all_to_all(sent.reshape(TILES * NEAR, CHUNK // 2, 2, 2 * ROWS), ('til...  22.4 us
    all_to_all x1, blocking collectives, per_device(): gathered = lax.all_to_all(copies, 'far', 0, 0, tiled=True)  10.2 us
    pallas_call x1, Pallas kernels, per_device(): call(apply_kernel, (shape((LEVELS, ROWS, N), BF16), shape((LEVELS, OWN, M...  2.44 us
    pallas_call x1, Pallas kernels, per_device(): call(project_kernel, shape((TILES, NEAR, OWN, 2 * ROWS), BF16), in_specs=...  2.31 us

profile of v4, /device:TPU:1, one launch (start us, length us, event | category | flops | bytes accessed | tf_op | source)
XLA Modules:
  0.0 72.1 jit_solution(2830217861749262094)
XLA Ops:
  0.6 0.0 copy-start.3
  0.6 0.0 copy-start.4
  0.7 0.0 copy-start.1
  0.7 0.0 copy-start.2
  0.7 0.0 copy-start.6
  0.7 0.0 copy-start.7
  0.7 2.3 %shard_map.104 = bf16[32,4,8,128]{3,2,1,0:T(8,128)(2,1)S(1)} custom-call(bf16[8,64,2048]{2,1,0:T(8,128)(2,1)} %bitcast.6, bf16[1024,256]{1,0:T(8,128)(2,1)} %constant.12.clone.by_ref), custom_call_target="tpu_custom_call" | custom-call | tf_op jit(solution)/shard_map/pallas_call | solution.py:206
  3.0 32.5 %all_to_all.15 = bf16[128,8,128]{2,1,0:T(8,128)(2,1)S(1)} all-to-all(bf16[128,8,128]{2,1,0:T(8,128)(2,1)S(1)} %bitcast.11), channel_id=1, replica_groups=mesh['far'=4,'near'=4,'tile'=32] {'tile','near'}, dimensions={0} | all-to-all | bytes 524288 | tf_op jit(solution)/shard_map/all_to_all | solution.py:218
  35.5 0.0 copy-done.3
  35.5 0.0 copy-done.4
  35.5 0.0 copy-start
  35.5 0.0 copy-start.5
  35.5 0.4 shard_map.105
  35.9 10.2 %all_to_all.16.all_ref = f32[4,64,256]{2,1,0:T(8,128)S(1)} all-to-all(f32[4,64,256]{2,1,0:T(8,128)S(1)} %get-tuple-element.6), channel_id=1, replica_groups=mesh['far'=4,'near'=4,'tile'=32] {'far'}, dimensions={0} | all-to-all | bytes 524288 | tf_op jit(solution)/shard_map/all_to_all | solution.py:228
  46.0 0.0 copy-done.1
  46.0 0.0 copy-done.2
  46.0 0.0 copy-done.6
  46.1 0.0 copy-done.7
  46.1 1.1 %shard_map.106 = bf16[1280,128]{1,0:T(8,128)(2,1)S(1)} custom-call(f32[4,64,256]{2,1,0:T(8,128)S(1)} %all_to_all.16.all_ref, f32[64,256]{1,0:T(8,128)S(1)} %get-tuple-element.7.own_ref, f32[8]{0:T(128)S(1)} %copy-done.6, f32[8]{0:T(128)S(1)} %copy-done.7, bf16[256,1024]{1,0:T(8,128)(2,1)S(1)} %copy-done.2, bf16[256,1024]{1,0:T(8,128)(2,1)S(1)} %copy-done.1), custom_call_target="tpu_custom_call" | custom-call | tf_op jit(solution)/shard_map/pallas_call | solution.py:229
  47.2 22.4 %all_to_all.17 = bf16[128,5,2,128]{3,2,1,0:T(2,128)(2,1)S(1)} all-to-all(bf16[128,5,2,128]{3,2,1,0:T(2,128)(2,1)S(1)} %bitcast.8), channel_id=1, replica_groups=mesh['far'=4,'near'=4,'tile'=32] {'tile','near'}, dimensions={0} | all-to-all | bytes 655360 | tf_op jit(solution)/shard_map/all_to_all | solution.py:235
  69.6 0.0 copy-done
  69.6 0.0 copy-done.5
  69.6 2.4 %shard_map.107 = (bf16[8,64,2048]{2,1,0:T(8,128)(2,1)}, f32[8,8,256]{2,1,0:T(8,128)}) custom-call(bf16[8,64,2048]{2,1,0:T(8,128)(2,1)S(1)} %bitcast.7, bf16[1280,128]{1,0:T(8,128)(2,1)S(1)} %bitcast.9, bf16[256,1024]{1,0:T(8,128)(2,1)S(1)} %copy-done.5), custom_call_target="tpu_custom_call" | custom-call | tf_op jit(solution)/shard_map/pallas_call | solution.py:238
Async XLA Ops:
  0.6 34.9 %copy-start.3 = (bf16[1024,256]{1,0:T(8,128)(2,1)S(1)}, bf16[1024,256]{1,0:T(8,128)(2,1)}, u32[]{:S(2)}) copy-start(bf16[1024,256]{1,0:T(8,128)(2,1)} %constant.14.clone.low_ref) | copy-start | bytes 1572868
  0.6 34.8 %copy-start.4 = (bf16[1024,256]{1,0:T(8,128)(2,1)S(1)}, bf16[1024,256]{1,0:T(8,128)(2,1)}, u32[]{:S(2)}) copy-start(bf16[1024,256]{1,0:T(8,128)(2,1)} %constant.13.clone.high_ref) | copy-start | bytes 1572868
  0.7 45.4 %copy-start.1 = (bf16[256,1024]{1,0:T(8,128)(2,1)S(1)}, bf16[256,1024]{1,0:T(8,128)(2,1)}, u32[]{:S(2)}) copy-start(bf16[256,1024]{1,0:T(8,128)(2,1)} %constant.16.clone.low_ref) | copy-start | bytes 1572868
  0.7 45.4 %copy-start.2 = (bf16[256,1024]{1,0:T(8,128)(2,1)S(1)}, bf16[256,1024]{1,0:T(8,128)(2,1)}, u32[]{:S(2)}) copy-start(bf16[256,1024]{1,0:T(8,128)(2,1)} %constant.15.clone.high_ref) | copy-start | bytes 1572868
  0.7 45.4 %copy-start.6 = (f32[8]{0:T(128)S(1)}, f32[8]{0:T(128)}, u32[]{:S(2)}) copy-start(f32[8]{0:T(128)} %obs_ref.1) | copy-start | bytes 100
  0.7 45.4 %copy-start.7 = (f32[8]{0:T(128)S(1)}, f32[8]{0:T(128)}, u32[]{:S(2)}) copy-start(f32[8]{0:T(128)} %relax_ref.1) | copy-start | bytes 100
  35.5 34.1 %copy-start = (bf16[1,8,64,2048]{3,2,1,0:T(8,128)(2,1)S(1)}, bf16[1,8,64,2048]{3,2,1,0:T(8,128)(2,1)}, u32[]{:S(2)}) copy-start(bf16[1,8,64,2048]{3,2,1,0:T(8,128)(2,1)} %param.9) | copy-start | bytes 6291460
  35.5 34.1 %copy-start.5 = (bf16[256,1024]{1,0:T(8,128)(2,1)S(1)}, bf16[256,1024]{1,0:T(8,128)(2,1)}, u32[]{:S(2)}) copy-start(bf16[256,1024]{1,0:T(8,128)(2,1)} %constant.17.clone.by_ref) | copy-start | bytes 1572868

commit v5 on v4

v5 whole, which is shorter than its diff:
```python
import functools
import math

import jax
import jax.numpy as jnp
import numpy as np
from jax import lax
from jax.experimental import pallas as pl
from jax.experimental.pallas import tpu as pltpu
from jax.sharding import Mesh, PartitionSpec as P

N = 2048
MODES = 256
LEVELS = 8
MEMBERS = 16
TILES = 32
ROWS = N // TILES
NEAR = 4
FAR = MEMBERS // NEAR
OWN = MODES // TILES
STEPS = 4
HALF = N // 2
WIDTH = HALF // STEPS
SLOTS = 32
RANK = 20
GROUP = 4
SIDE = MODES // GROUP
CHUNK = GROUP + 2
PART = NEAR * GROUP
MIB = 1024 * 1024
BF16 = jnp.bfloat16
F32 = jnp.float32


def mode_table():
    mode = np.arange(MODES)[None, :]
    phases = (np.arange(N)[:, None] * ((mode + 1) // 2)) % N
    angles = 2.0 * math.pi / N * phases
    scaled = np.where(mode % 2 == 1, np.sin(angles), np.cos(angles))
    factor = np.where(mode == 0, math.sqrt(1.0 / N), math.sqrt(2.0 / N))
    return scaled * factor


def row_basis():
    n = np.arange(ROWS)
    centre = ((ROWS - 1 - 2 * n) / 2.0) ** 2 * math.cos(math.pi * MODES / N)
    beside = n[1:] * (ROWS - n[1:]) / 2.0
    vectors = np.linalg.eigh(np.diag(centre) + np.diag(beside, 1) + np.diag(beside, -1))[1]
    basis = vectors[:, ::-1][:, :RANK]
    return basis * np.sign(basis[0])


def split(table):
    high = table.astype(np.float32).astype(BF16)
    return high, (table - high.astype(np.float64)).astype(np.float32).astype(BF16)


def tables():
    full = mode_table()
    flip = lambda a: np.ascontiguousarray(a.T)
    first = np.arange(MODES).reshape(TILES, OWN).T.reshape(-1)
    second = np.arange(MODES).reshape(GROUP, SIDE).T.reshape(-1)
    slots = np.concatenate([np.arange(RANK), np.arange(SLOTS - RANK)])
    basis = row_basis()
    blocks = full.reshape(TILES, ROWS, MODES)
    modes = np.stack(
        [(blocks * basis[:, k][None, :, None]).sum(axis=1) for k in range(RANK)], axis=1
    )
    bx_high, bx_low = split(modes[:, slots][:, :, first].reshape(TILES * SLOTS, MODES))
    narrow = np.kron(np.eye(GROUP), basis[:, slots].T)
    narrow_high, narrow_low = split(narrow)
    by = full[:HALF].astype(np.float32).astype(BF16)[:, second]
    narrow_both = np.concatenate([narrow_high, narrow_low], axis=0)
    spread_both = np.concatenate([flip(narrow_high), flip(narrow_low)], axis=0)
    return bx_high, bx_low, flip(bx_high), flip(bx_low), by, flip(by), narrow_both, spread_both


def signs(major, minor):
    column = lax.broadcasted_iota(jnp.int32, (1, MODES), 1)
    mode = major * (column % minor) + column // minor
    return (1 - 2 * ((mode + 1) // 2 % 2)).astype(F32)


def dot(a, b, dims):
    return lax.dot_general(a, b, (dims, ((), ())), preferred_element_type=F32)


def parts(values):
    high = values.astype(BF16)
    return high, (values - high.astype(F32)).astype(BF16)


def low_slots(values, axis):
    slot = lax.broadcasted_iota(jnp.int32, values.shape, axis) % SLOTS
    rounded = values.astype(BF16).astype(F32)
    return jnp.where(slot < RANK, rounded, values - rounded)


def project_kernel(states_ref, by_ref, narrow_ref, out_ref, field, table, small, acc, sems):
    last = pltpu.make_async_copy(narrow_ref, small, sems.at[3 * STEPS])

    def copies(k):
        rows = pl.ds(WIDTH * k, WIDTH)
        yield pltpu.make_async_copy(by_ref.at[rows, :], table.at[k], sems.at[3 * k])
        for h in range(2):
            cols = pl.ds(HALF * h + WIDTH * k, WIDTH)
            yield pltpu.make_async_copy(
                states_ref.at[:, :, cols], field.at[k, h], sems.at[3 * k + 1 + h]
            )

    for k in range(STEPS):
        for c in copies(k):
            c.start()
    last.start()
    for k in range(STEPS):
        for c in copies(k):
            c.wait()
        for h in range(2):
            part = dot(field[k, h].reshape(LEVELS * ROWS, WIDTH), table[k], ((1,), (0,)))
            rows = slice(LEVELS * ROWS * h, LEVELS * ROWS * (h + 1))
            acc[rows, :] = part if k == 0 else acc[rows, :] + part
    last.wait()
    sign = signs(SIDE, GROUP)
    count = GROUP * SLOTS
    sides = []
    for c in range(2):
        lower = acc[GROUP * ROWS * c : GROUP * ROWS * (c + 1), :]
        upper = acc[GROUP * ROWS * (c + 2) : GROUP * ROWS * (c + 3), :]
        high, low = parts(lower + sign * upper)
        both = dot(small[...], high, ((1,), (0,)))
        narrow = both[:count] + both[count:] + dot(small[:count, :], low, ((1,), (0,)))
        sides.append(low_slots(narrow, 0).T)
    for r in range(SIDE // 2):
        rows = []
        for k in range(2):
            for side in sides:
                rows.append(side[GROUP * (2 * r + k) : GROUP * (2 * r + k + 1)])
        out_ref[4 * GROUP * r : 4 * GROUP * (r + 1), :] = jnp.concatenate(rows, axis=0).astype(BF16)


def coeffs_kernel(rows_ref, high_ref, low_ref, out_ref, copies_ref, wide):
    lanes = GROUP * SLOTS
    for u in range(TILES // GROUP):
        pieces = [rows_ref[PART * (GROUP * u + k) : PART * (GROUP * u + k + 1), :] for k in range(GROUP)]
        for l in range(GROUP):
            wide[PART * l : PART * (l + 1), lanes * u : lanes * (u + 1)] = jnp.concatenate(
                [p[:, SLOTS * l : SLOTS * (l + 1)] for p in pieces], axis=1
            )
    x = wide[...]
    coeffs = dot(x, high_ref[...], ((1,), (0,))) + dot(x, low_ref[...], ((1,), (0,)))
    coeffs = swap_rows(coeffs)
    out_ref[...] = coeffs
    for k in range(FAR):
        copies_ref[k] = coeffs


def swap_rows(values):
    return jnp.concatenate(
        [
            values[PART * l + GROUP * k : PART * l + GROUP * (k + 1)]
            for k in range(GROUP)
            for l in range(NEAR)
        ],
        axis=0,
    )


def nudge_kernel(all_ref, own_ref, obs_ref, relax_ref, high_ref, low_ref, sent_ref):
    base = GROUP * (lax.axis_index("near") % 2)
    level = lax.broadcasted_iota(jnp.int32, (PART, MODES), 0) // GROUP
    obs = jnp.zeros((PART, MODES), F32)
    relax = jnp.zeros((PART, MODES), F32)
    for l in range(GROUP):
        obs = jnp.where(level == l, obs_ref[base + l], obs)
        relax = jnp.where(level == l, relax_ref[base + l], relax)
    members = [slice(PART * k, PART * (k + 1)) for k in range(NEAR)]
    driver = all_ref[0, members[0], :]
    departures = [all_ref[f, m, :] - driver for f in range(FAR) for m in members]
    mean = sum(departures[1:], departures[0]) * (1.0 / MEMBERS)
    squares = [(d - mean) * (d - mean) for d in departures]
    spread = sum(squares[1:], squares[0]) * (1.0 / MEMBERS)
    gain = relax * spread / (spread + obs)
    misfit = jnp.concatenate([-gain * (own_ref[m, :] - driver) for m in members], axis=0)
    high, low = parts(swap_rows(misfit))
    count = NEAR * PART
    both = dot(jnp.concatenate([high, low], axis=0), high_ref[...], ((1,), (0,)))
    back = both[:count] + both[count:] + dot(high, low_ref[...], ((1,), (0,)))
    back = low_slots(back, 1)
    stacked = jnp.concatenate(
        [spread[:, TILES * k : TILES * (k + 1)] for k in range(OWN)], axis=0
    ).T
    first = stacked.astype(BF16).astype(F32)
    second = stacked - first
    for t in range(TILES):
        cols = slice(SLOTS * t, SLOTS * (t + 1))
        rows = jnp.concatenate([back[PART * l : PART * (l + 1), cols] for l in range(GROUP)], axis=1)
        extra = jnp.concatenate([first[t : t + 1], second[t : t + 1]], axis=0)
        pieces = []
        for k in range(NEAR):
            pieces += [rows[GROUP * k : GROUP * (k + 1)], extra]
        sent_ref[NEAR * CHUNK * t : NEAR * CHUNK * (t + 1), :] = jnp.concatenate(
            pieces, axis=0
        ).astype(BF16)


def apply_kernel(
    states_ref, got_ref, by_ref, wide_ref, out_ref, spread_ref, back, filled, mixed, turned, sems
):
    def copy(c, h):
        part = (pl.ds(GROUP * c, GROUP), slice(None), pl.ds(HALF * h, HALF))
        return pltpu.make_async_copy(filled.at[part], out_ref.at[part], sems.at[2 * c + h])

    for t in range(TILES):
        rows = got_ref[NEAR * CHUNK * t : NEAR * CHUNK * (t + 1), :].astype(F32)
        for k in range(NEAR):
            piece = rows[CHUNK * k : CHUNK * (k + 1)]
            r, c = 2 * t + k // 2, k % 2
            back[c, GROUP * r : GROUP * (r + 1), :] = piece[:GROUP]
            mixed[SIDE * c + r : SIDE * c + r + 1, :] = piece[GROUP : GROUP + 1] + piece[GROUP + 1 :]
    sign = signs(SIDE, GROUP).astype(BF16)
    count = GROUP * ROWS
    for c in range(2):
        both = dot(wide_ref[...], back[c].astype(BF16).T, ((1,), (0,)))
        modes = (both[:count] + both[count:]).astype(BF16)
        for h in range(2):
            cols = slice(HALF * h, HALF * (h + 1))
            increment = dot(modes if h == 0 else modes * sign, by_ref[...], ((1,), (0,)))
            field = states_ref[GROUP * c : GROUP * (c + 1), :, cols].astype(F32)
            total = field + increment.reshape(GROUP, ROWS, HALF)
            filled[GROUP * c : GROUP * (c + 1), :, cols] = total.astype(BF16)
            copy(c, h).start()
    turned[...] = mixed[...].T
    for l in range(GROUP):
        strips = [turned[pl.ds(GROUP * l + k, OWN, stride=PART), :] for k in range(GROUP)]
        for c in range(2):
            spread_ref[GROUP * c + l] = jnp.concatenate(
                [s[:, SIDE * c : SIDE * (c + 1)] for s in strips], axis=1
            )
    for c in range(2):
        for h in range(2):
            copy(c, h).wait()


def call(kernel, outs, limit=24 * MIB, **kw):
    return pl.pallas_call(
        kernel,
        out_shape=outs,
        compiler_params=pltpu.CompilerParams(vmem_limit_bytes=limit),
        **kw,
    )


def shape(dims, dtype):
    return jax.ShapeDtypeStruct(dims, dtype)


def per_device(consts, states, obs_var, relax_rate):
    bx_high, bx_low, bx_high_t, bx_low_t, by, by_t, narrow, widen = consts
    field = states[0]
    hbm = pl.BlockSpec(memory_space=pltpu.HBM)
    smem = pl.BlockSpec(memory_space=pltpu.SMEM)
    vmem = pl.BlockSpec(memory_space=pltpu.VMEM)
    devices, lanes, columns = TILES * NEAR, GROUP * SLOTS, NEAR * PART

    def exchange(rows):
        chunks = rows.reshape(devices, rows.shape[0] // (2 * devices), 2, lanes)
        return lax.all_to_all(chunks, ("tile", "near"), 0, 0, tiled=True).reshape(rows.shape)

    sent = call(
        project_kernel,
        shape((devices * GROUP, lanes), BF16),
        in_specs=[hbm] * 3,
        out_specs=vmem,
        scratch_shapes=[
            pltpu.VMEM((STEPS, 2, LEVELS, ROWS, WIDTH), BF16),
            pltpu.VMEM((STEPS, WIDTH, MODES), BF16),
            pltpu.VMEM((2 * lanes, GROUP * ROWS), BF16),
            pltpu.VMEM((2 * LEVELS * ROWS, MODES), F32),
            pltpu.SemaphoreType.DMA((3 * STEPS + 1,)),
        ],
    )(*(pltpu.with_memory_space_constraint(x, pltpu.HBM) for x in (field, by, narrow)))
    coeffs, copies = call(
        coeffs_kernel,
        (shape((columns, MODES), F32), shape((FAR, columns, MODES), F32)),
        in_specs=[vmem] * 3,
        out_specs=(vmem, vmem),
        scratch_shapes=[pltpu.VMEM((columns, TILES * SLOTS), BF16)],
    )(exchange(sent), bx_high, bx_low)
    gathered = lax.all_to_all(copies, "far", 0, 0, tiled=True)
    sent = call(
        nudge_kernel,
        shape((devices * CHUNK, lanes), BF16),
        in_specs=[vmem, vmem, smem, smem, vmem, vmem],
        out_specs=vmem,
    )(gathered, coeffs, obs_var, relax_rate, bx_high_t, bx_low_t)
    nudged, spread = call(
        apply_kernel,
        (shape((LEVELS, ROWS, N), BF16), shape((LEVELS, OWN, MODES), F32)),
        in_specs=[vmem] * 4,
        out_specs=(hbm, vmem),
        scratch_shapes=[
            pltpu.VMEM((2, MODES, lanes), F32),
            pltpu.VMEM((LEVELS, ROWS, N), BF16),
            pltpu.VMEM((2 * SIDE, lanes), F32),
            pltpu.VMEM((lanes, 2 * SIDE), F32),
            pltpu.SemaphoreType.DMA((4,)),
        ],
    )(field, exchange(sent), by_t, widen)
    return nudged[None], spread


def solution(mesh):
    fine = Mesh(mesh.devices.reshape(FAR, NEAR, TILES), ("far", "near", "tile"))
    rows = P(("far", "near"), None, "tile", None)
    return jax.shard_map(
        functools.partial(per_device, tables()),
        mesh=fine,
        in_specs=(rows, P(), P()),
        out_specs=(rows, P(None, "tile", None)),
        check_vma=False,
    )
```

time: 72.3 us -> 67.6 us (0.935)
  blocking collectives: 65.1 us -> 59.8 us
    all_to_all x2, blocking collectives: 54.9 us -> 50.2 us  [exchange(): lax.all_to_all(chunks, ('tile', 'near'), 0, 0, tiled=True)]
where the time goes in v5:
time: 67.6 us; the launch traced here: 67.4 us
  blocking collectives  59.8 us (88%)
  Pallas kernels  6.82 us (10%)
  between operations  0.74 us (1%)
    all_to_all x2, blocking collectives, exchange(): lax.all_to_all(chunks, ('tile', 'near'), 0, 0, tiled=True)  50.2 us
    all_to_all x1, blocking collectives, per_device(): gathered = lax.all_to_all(copies, 'far', 0, 0, tiled=True)  9.61 us
    pallas_call x1, Pallas kernels, per_device(): call(apply_kernel, (shape((LEVELS, ROWS, N), BF16), shape((LEVELS, OWN, M...  2.7 us
    pallas_call x1, Pallas kernels, per_device(): call(project_kernel, shape((devices * GROUP, lanes), BF16), in_specs=[hbm...  2.66 us

profile of v5, /device:TPU:1, one launch (start us, length us, event | category | flops | bytes accessed | tf_op | source)
XLA Modules:
  0.0 67.4 jit_solution(5668915555895732557)
XLA Ops:
  0.6 0.0 copy-start.1
  0.6 0.0 copy-start.2
  0.7 0.0 copy-start.4
  0.7 0.0 copy-start.5
  0.7 0.0 copy-start.7
  0.7 0.0 copy-start.8
  0.7 2.7 %shard_map.122 = bf16[512,128]{1,0:T(8,128)(2,1)S(1)} custom-call(bf16[8,64,2048]{2,1,0:T(8,128)(2,1)} %bitcast.6, bf16[1024,256]{1,0:T(8,128)(2,1)} %constant.16.clone.by_ref, bf16[256,256]{1,0:T(8,128)(2,1)} %constant.17.clone.narrow_ref), custom_call_target="tpu_custom_call" | custom-call | tf_op jit(solution)/shard_map/pallas_call | solution.py:269
  3.4 0.0 copy-start
  3.4 0.0 copy-start.3
  3.4 0.0 copy-start.6
  3.4 30.4 %all_to_all.15 = bf16[128,2,2,128]{3,2,1,0:T(2,128)(2,1)S(1)} all-to-all(bf16[128,2,2,128]{3,2,1,0:T(2,128)(2,1)S(1)} %bitcast.11), channel_id=1, replica_groups=mesh['far'=4,'near'=4,'tile'=32] {'tile','near'}, dimensions={0} | all-to-all | bytes 262144 | tf_op jit(solution)/shard_map/all_to_all | solution.py:267
  33.8 0.0 copy-done.1
  33.8 0.0 copy-done.2
  33.8 0.4 shard_map.123
  34.2 9.6 %all_to_all.16.all_ref = f32[4,64,256]{2,1,0:T(8,128)S(1)} all-to-all(f32[4,64,256]{2,1,0:T(8,128)S(1)} %get-tuple-element.6), channel_id=1, replica_groups=mesh['far'=4,'near'=4,'tile'=32] {'far'}, dimensions={0} | all-to-all | bytes 524288 | tf_op jit(solution)/shard_map/all_to_all | solution.py:289
  43.8 0.0 copy-done.4
  43.8 0.0 copy-done.5
  43.8 0.0 copy-done.7
  43.8 0.0 copy-done.8
  43.8 1.1 %shard_map.124 = bf16[768,128]{1,0:T(8,128)(2,1)S(1)} custom-call(f32[4,64,256]{2,1,0:T(8,128)S(1)} %all_to_all.16.all_ref, f32[64,256]{1,0:T(8,128)S(1)} %get-tuple-element.7.own_ref, f32[8]{0:T(128)S(1)} %copy-done.7, f32[8]{0:T(128)S(1)} %copy-done.8, bf16[256,1024]{1,0:T(8,128)(2,1)S(1)} %copy-done.5, bf16[256,1024]{1,0:T(8,128)(2,1)S(1)} %copy-done.4), custom_call_target="tpu_custom_call" | custom-call | tf_op jit(solution)/shard_map/pallas_call | solution.py:290
  44.9 19.8 %all_to_all.17 = bf16[128,3,2,128]{3,2,1,0:T(2,128)(2,1)S(1)} all-to-all(bf16[128,3,2,128]{3,2,1,0:T(2,128)(2,1)S(1)} %bitcast.9), channel_id=1, replica_groups=mesh['far'=4,'near'=4,'tile'=32] {'tile','near'}, dimensions={0} | all-to-all | bytes 393216 | tf_op jit(solution)/shard_map/all_to_all | solution.py:267
  64.7 0.0 copy-done
  64.7 0.0 copy-done.3
  64.7 0.0 copy-done.6
  64.7 2.7 %shard_map.125 = (bf16[8,64,2048]{2,1,0:T(8,128)(2,1)}, f32[8,8,256]{2,1,0:T(8,128)}) custom-call(bf16[8,64,2048]{2,1,0:T(8,128)(2,1)S(1)} %bitcast.7, bf16[768,128]{1,0:T(8,128)(2,1)S(1)} %bitcast.8, bf16[256,1024]{1,0:T(8,128)(2,1)S(1)} %copy-done.3, bf16[512,128]{1,0:T(8,128)(2,1)S(1)} %copy-done.6), custom_call_target="tpu_custom_call" | custom-call | tf_op jit(solution)/shard_map/pallas_call | solution.py:296
Async XLA Ops:
  0.6 33.2 %copy-start.1 = (bf16[1024,256]{1,0:T(8,128)(2,1)S(1)}, bf16[1024,256]{1,0:T(8,128)(2,1)}, u32[]{:S(2)}) copy-start(bf16[1024,256]{1,0:T(8,128)(2,1)} %constant.19.clone.low_ref) | copy-start | bytes 1572868
  0.6 33.2 %copy-start.2 = (bf16[1024,256]{1,0:T(8,128)(2,1)S(1)}, bf16[1024,256]{1,0:T(8,128)(2,1)}, u32[]{:S(2)}) copy-start(bf16[1024,256]{1,0:T(8,128)(2,1)} %constant.18.clone.high_ref) | copy-start | bytes 1572868
  0.7 43.1 %copy-start.4 = (bf16[256,1024]{1,0:T(8,128)(2,1)S(1)}, bf16[256,1024]{1,0:T(8,128)(2,1)}, u32[]{:S(2)}) copy-start(bf16[256,1024]{1,0:T(8,128)(2,1)} %constant.21.clone.low_ref) | copy-start | bytes 1572868
  0.7 43.1 %copy-start.5 = (bf16[256,1024]{1,0:T(8,128)(2,1)S(1)}, bf16[256,1024]{1,0:T(8,128)(2,1)}, u32[]{:S(2)}) copy-start(bf16[256,1024]{1,0:T(8,128)(2,1)} %constant.20.clone.high_ref) | copy-start | bytes 1572868
  0.7 43.1 %copy-start.7 = (f32[8]{0:T(128)S(1)}, f32[8]{0:T(128)}, u32[]{:S(2)}) copy-start(f32[8]{0:T(128)} %obs_ref.1) | copy-start | bytes 100
  0.7 43.1 %copy-start.8 = (f32[8]{0:T(128)S(1)}, f32[8]{0:T(128)}, u32[]{:S(2)}) copy-start(f32[8]{0:T(128)} %relax_ref.1) | copy-start | bytes 100
  3.4 61.3 %copy-start = (bf16[1,8,64,2048]{3,2,1,0:T(8,128)(2,1)S(1)}, bf16[1,8,64,2048]{3,2,1,0:T(8,128)(2,1)}, u32[]{:S(2)}) copy-start(bf16[1,8,64,2048]{3,2,1,0:T(8,128)(2,1)} %param.11) | copy-start | bytes 6291460
  3.4 61.3 %copy-start.3 = (bf16[256,1024]{1,0:T(8,128)(2,1)S(1)}, bf16[256,1024]{1,0:T(8,128)(2,1)}, u32[]{:S(2)}) copy-start(bf16[256,1024]{1,0:T(8,128)(2,1)} %constant.22.clone.by_ref) | copy-start | bytes 1572868
  3.4 61.3 %copy-start.6 = (bf16[512,128]{1,0:T(8,128)(2,1)S(1)}, bf16[512,128]{1,0:T(8,128)(2,1)}, u32[]{:S(2)}) copy-start(bf16[512,128]{1,0:T(8,128)(2,1)} %constant.23.clone.wide_ref) | copy-start | bytes 393220

commit v6 on v5

--- a/solution.py
+++ b/solution.py
@@ -167,12 +167,10 @@
 
 def nudge_kernel(all_ref, own_ref, obs_ref, relax_ref, high_ref, low_ref, sent_ref):
     base = GROUP * (lax.axis_index("near") % 2)
-    level = lax.broadcasted_iota(jnp.int32, (PART, MODES), 0) // GROUP
-    obs = jnp.zeros((PART, MODES), F32)
-    relax = jnp.zeros((PART, MODES), F32)
-    for l in range(GROUP):
-        obs = jnp.where(level == l, obs_ref[base + l], obs)
-        relax = jnp.where(level == l, relax_ref[base + l], relax)
+    level = base + lax.broadcasted_iota(jnp.int32, (PART, LEVELS), 0) // GROUP
+    here = level == lax.broadcasted_iota(jnp.int32, (PART, LEVELS), 1)
+    obs = jnp.sum(jnp.where(here, obs_ref[...], 0.0), axis=1, keepdims=True)
+    relax = jnp.sum(jnp.where(here, relax_ref[...], 0.0), axis=1, keepdims=True)
     members = [slice(PART * k, PART * (k + 1)) for k in range(NEAR)]
     driver = all_ref[0, members[0], :]
     departures = [all_ref[f, m, :] - driver for f in range(FAR) for m in members]
@@ -204,7 +202,7 @@
 
 
 def apply_kernel(
-    states_ref, got_ref, by_ref, wide_ref, out_ref, spread_ref, back, filled, mixed, turned, sems
+    states_ref, got_ref, by_ref, wide_ref, out_ref, spread_ref, back, filled, mixed, turned, variance, sems
 ):
     def copy(c, h):
         part = (pl.ds(GROUP * c, GROUP), slice(None), pl.ds(HALF * h, HALF))
@@ -213,13 +211,26 @@
     for t in range(TILES):
         rows = got_ref[NEAR * CHUNK * t : NEAR * CHUNK * (t + 1), :].astype(F32)
         for k in range(NEAR):
-            piece = rows[CHUNK * k : CHUNK * (k + 1)]
-            r, c = 2 * t + k // 2, k % 2
-            back[c, GROUP * r : GROUP * (r + 1), :] = piece[:GROUP]
-            mixed[SIDE * c + r : SIDE * c + r + 1, :] = piece[GROUP : GROUP + 1] + piece[GROUP + 1 :]
+            row = SIDE * (k % 2) + 2 * t + k // 2
+            extra = rows[CHUNK * k + GROUP : CHUNK * (k + 1)]
+            mixed[row : row + 1, :] = extra[:1] + extra[1:]
+    turned[...] = mixed[...].T
+    for l in range(GROUP):
+        strips = [turned[pl.ds(GROUP * l + k, OWN, stride=PART), :] for k in range(GROUP)]
+        for c in range(2):
+            variance[GROUP * c + l] = jnp.concatenate(
+                [s[:, SIDE * c : SIDE * (c + 1)] for s in strips], axis=1
+            )
+    last = pltpu.make_async_copy(variance, spread_ref, sems.at[4])
+    last.start()
     sign = signs(SIDE, GROUP).astype(BF16)
     count = GROUP * ROWS
     for c in range(2):
+        for t in range(TILES):
+            rows = got_ref[NEAR * CHUNK * t : NEAR * CHUNK * (t + 1), :].astype(F32)
+            for k in range(2):
+                r, row = 2 * t + k, CHUNK * (2 * k + c)
+                back[c, GROUP * r : GROUP * (r + 1), :] = rows[row : row + GROUP]
         both = dot(wide_ref[...], back[c].astype(BF16).T, ((1,), (0,)))
         modes = (both[:count] + both[count:]).astype(BF16)
         for h in range(2):
@@ -229,16 +240,10 @@
             total = field + increment.reshape(GROUP, ROWS, HALF)
             filled[GROUP * c : GROUP * (c + 1), :, cols] = total.astype(BF16)
             copy(c, h).start()
-    turned[...] = mixed[...].T
-    for l in range(GROUP):
-        strips = [turned[pl.ds(GROUP * l + k, OWN, stride=PART), :] for k in range(GROUP)]
-        for c in range(2):
-            spread_ref[GROUP * c + l] = jnp.concatenate(
-                [s[:, SIDE * c : SIDE * (c + 1)] for s in strips], axis=1
-            )
     for c in range(2):
         for h in range(2):
             copy(c, h).wait()
+    last.wait()
 
 
 def call(kernel, outs, limit=24 * MIB, **kw):
@@ -258,7 +263,6 @@
     bx_high, bx_low, bx_high_t, bx_low_t, by, by_t, narrow, widen = consts
     field = states[0]
     hbm = pl.BlockSpec(memory_space=pltpu.HBM)
-    smem = pl.BlockSpec(memory_space=pltpu.SMEM)
     vmem = pl.BlockSpec(memory_space=pltpu.VMEM)
     devices, lanes, columns = TILES * NEAR, GROUP * SLOTS, NEAR * PART
 
@@ -290,20 +294,21 @@
     sent = call(
         nudge_kernel,
         shape((devices * CHUNK, lanes), BF16),
-        in_specs=[vmem, vmem, smem, smem, vmem, vmem],
+        in_specs=[vmem] * 6,
         out_specs=vmem,
-    )(gathered, coeffs, obs_var, relax_rate, bx_high_t, bx_low_t)
+    )(gathered, coeffs, obs_var[None], relax_rate[None], bx_high_t, bx_low_t)
     nudged, spread = call(
         apply_kernel,
         (shape((LEVELS, ROWS, N), BF16), shape((LEVELS, OWN, MODES), F32)),
         in_specs=[vmem] * 4,
-        out_specs=(hbm, vmem),
+        out_specs=(hbm, hbm),
         scratch_shapes=[
             pltpu.VMEM((2, MODES, lanes), F32),
             pltpu.VMEM((LEVELS, ROWS, N), BF16),
             pltpu.VMEM((2 * SIDE, lanes), F32),
             pltpu.VMEM((lanes, 2 * SIDE), F32),
-            pltpu.SemaphoreType.DMA((4,)),
+            pltpu.VMEM((LEVELS, OWN, MODES), F32),
+            pltpu.SemaphoreType.DMA((5,)),
         ],
     )(field, exchange(sent), by_t, widen)
     return nudged[None], spread

time: 67.6 us -> 66.4 us (0.982)
  Pallas kernels: 6.82 us -> 5.62 us
where the time goes in v6:
time: 66.4 us; the launch traced here: 66.2 us
  blocking collectives  59.8 us (90%)
  Pallas kernels  5.62 us (8%)
  between operations  0.74 us (1%)
    all_to_all x2, blocking collectives, exchange(): lax.all_to_all(chunks, ('tile', 'near'), 0, 0, tiled=True)  50.1 us
    all_to_all x1, blocking collectives, per_device(): gathered = lax.all_to_all(copies, 'far', 0, 0, tiled=True)  9.61 us
    pallas_call x1, Pallas kernels, per_device(): call(project_kernel, shape((devices * GROUP, lanes), BF16), in_specs=[hbm...  2.66 us
    pallas_call x1, Pallas kernels, per_device(): call(apply_kernel, (shape((LEVELS, ROWS, N), BF16), shape((LEVELS, OWN, M...  2.04 us

profile of v6, /device:TPU:1, one launch (start us, length us, event | category | flops | bytes accessed | tf_op | source)
XLA Modules:
  0.0 66.2 jit_solution(7832319038510540666)
XLA Ops:
  0.6 0.0 copy-start.1
  0.6 0.0 copy-start.2
  0.7 0.0 copy-start.4
  0.7 0.0 copy-start.5
  0.7 0.0 copy-start.7
  0.7 0.0 copy-start.8
  0.7 2.7 %shard_map.122 = bf16[512,128]{1,0:T(8,128)(2,1)S(1)} custom-call(bf16[8,64,2048]{2,1,0:T(8,128)(2,1)} %bitcast.8, bf16[1024,256]{1,0:T(8,128)(2,1)} %constant.16.clone.by_ref, bf16[256,256]{1,0:T(8,128)(2,1)} %constant.17.clone.narrow_ref), custom_call_target="tpu_custom_call" | custom-call | tf_op jit(solution)/shard_map/pallas_call | solution.py:273
  3.4 0.0 copy-start
  3.4 0.0 copy-start.3
  3.4 0.0 copy-start.6
  3.4 30.4 %all_to_all.15 = bf16[128,2,2,128]{3,2,1,0:T(2,128)(2,1)S(1)} all-to-all(bf16[128,2,2,128]{3,2,1,0:T(2,128)(2,1)S(1)} %bitcast.13), channel_id=1, replica_groups=mesh['far'=4,'near'=4,'tile'=32] {'tile','near'}, dimensions={0} | all-to-all | bytes 262144 | tf_op jit(solution)/shard_map/all_to_all | solution.py:271
  33.8 0.0 copy-done.1
  33.8 0.0 copy-done.2
  33.8 0.4 shard_map.123
  34.2 9.6 %all_to_all.16.all_ref = f32[4,64,256]{2,1,0:T(8,128)S(1)} all-to-all(f32[4,64,256]{2,1,0:T(8,128)S(1)} %get-tuple-element.6), channel_id=1, replica_groups=mesh['far'=4,'near'=4,'tile'=32] {'far'}, dimensions={0} | all-to-all | bytes 524288 | tf_op jit(solution)/shard_map/all_to_all | solution.py:293
  43.8 0.0 copy-done.4
  43.8 0.0 copy-done.5
  43.8 0.0 copy-done.7
  43.8 0.0 copy-done.8
  43.8 0.5 shard_map.124
  44.4 19.8 %all_to_all.17 = bf16[128,3,2,128]{3,2,1,0:T(2,128)(2,1)S(1)} all-to-all(bf16[128,3,2,128]{3,2,1,0:T(2,128)(2,1)S(1)} %bitcast.11), channel_id=1, replica_groups=mesh['far'=4,'near'=4,'tile'=32] {'tile','near'}, dimensions={0} | all-to-all | bytes 393216 | tf_op jit(solution)/shard_map/all_to_all | solution.py:271
  64.1 0.0 copy-done
  64.1 0.0 copy-done.3
  64.1 0.0 copy-done.6
  64.1 2.0 %shard_map.125 = (bf16[8,64,2048]{2,1,0:T(8,128)(2,1)}, f32[8,8,256]{2,1,0:T(8,128)}) custom-call(bf16[8,64,2048]{2,1,0:T(8,128)(2,1)S(1)} %bitcast.9, bf16[768,128]{1,0:T(8,128)(2,1)S(1)} %bitcast.10, bf16[256,1024]{1,0:T(8,128)(2,1)S(1)} %copy-done.3, bf16[512,128]{1,0:T(8,128)(2,1)S(1)} %copy-done.6), custom_call_target="tpu_custom_call" | custom-call | tf_op jit(solution)/shard_map/pallas_call | solution.py:300
Async XLA Ops:
  0.6 33.2 %copy-start.1 = (bf16[1024,256]{1,0:T(8,128)(2,1)S(1)}, bf16[1024,256]{1,0:T(8,128)(2,1)}, u32[]{:S(2)}) copy-start(bf16[1024,256]{1,0:T(8,128)(2,1)} %constant.19.clone.low_ref) | copy-start | bytes 1572868
  0.6 33.2 %copy-start.2 = (bf16[1024,256]{1,0:T(8,128)(2,1)S(1)}, bf16[1024,256]{1,0:T(8,128)(2,1)}, u32[]{:S(2)}) copy-start(bf16[1024,256]{1,0:T(8,128)(2,1)} %constant.18.clone.high_ref) | copy-start | bytes 1572868
  0.7 43.1 %copy-start.4 = (bf16[256,1024]{1,0:T(8,128)(2,1)S(1)}, bf16[256,1024]{1,0:T(8,128)(2,1)}, u32[]{:S(2)}) copy-start(bf16[256,1024]{1,0:T(8,128)(2,1)} %constant.21.clone.low_ref) | copy-start | bytes 1572868
  0.7 43.1 %copy-start.5 = (bf16[256,1024]{1,0:T(8,128)(2,1)S(1)}, bf16[256,1024]{1,0:T(8,128)(2,1)}, u32[]{:S(2)}) copy-start(bf16[256,1024]{1,0:T(8,128)(2,1)} %constant.20.clone.high_ref) | copy-start | bytes 1572868
  0.7 43.1 %copy-start.7 = (f32[8]{0:T(128)S(1)}, f32[8]{0:T(128)}, u32[]{:S(2)}) copy-start(f32[8]{0:T(128)} %param.12) | copy-start | bytes 100
  0.7 43.1 %copy-start.8 = (f32[8]{0:T(128)S(1)}, f32[8]{0:T(128)}, u32[]{:S(2)}) copy-start(f32[8]{0:T(128)} %param.13) | copy-start | bytes 100
  3.4 60.8 %copy-start = (bf16[1,8,64,2048]{3,2,1,0:T(8,128)(2,1)S(1)}, bf16[1,8,64,2048]{3,2,1,0:T(8,128)(2,1)}, u32[]{:S(2)}) copy-start(bf16[1,8,64,2048]{3,2,1,0:T(8,128)(2,1)} %param.11) | copy-start | bytes 6291460
  3.4 60.8 %copy-start.3 = (bf16[256,1024]{1,0:T(8,128)(2,1)S(1)}, bf16[256,1024]{1,0:T(8,128)(2,1)}, u32[]{:S(2)}) copy-start(bf16[256,1024]{1,0:T(8,128)(2,1)} %constant.22.clone.by_ref) | copy-start | bytes 1572868
  3.4 60.7 %copy-start.6 = (bf16[512,128]{1,0:T(8,128)(2,1)S(1)}, bf16[512,128]{1,0:T(8,128)(2,1)}, u32[]{:S(2)}) copy-start(bf16[512,128]{1,0:T(8,128)(2,1)} %constant.23.clone.wide_ref) | copy-start | bytes 393220

commit v7 on v6

--- a/solution.py
+++ b/solution.py
@@ -25,7 +25,7 @@
 RANK = 20
 GROUP = 4
 SIDE = MODES // GROUP
-CHUNK = GROUP + 2
+KEPT = SLOTS - OWN
 PART = NEAR * GROUP
 MIB = 1024 * 1024
 BF16 = jnp.bfloat16
@@ -67,12 +67,15 @@
         [(blocks * basis[:, k][None, :, None]).sum(axis=1) for k in range(RANK)], axis=1
     )
     bx_high, bx_low = split(modes[:, slots][:, :, first].reshape(TILES * SLOTS, MODES))
+    kept = (np.arange(SLOTS) < KEPT).astype(np.float64)
+    returned = (modes[:, slots] * kept[:, None])[:, :, first].reshape(TILES * SLOTS, MODES)
+    back_high, back_low = split(flip(returned))
     narrow = np.kron(np.eye(GROUP), basis[:, slots].T)
     narrow_high, narrow_low = split(narrow)
     by = full[:HALF].astype(np.float32).astype(BF16)[:, second]
     narrow_both = np.concatenate([narrow_high, narrow_low], axis=0)
-    spread_both = np.concatenate([flip(narrow_high), flip(narrow_low)], axis=0)
-    return bx_high, bx_low, flip(bx_high), flip(bx_low), by, flip(by), narrow_both, spread_both
+    wide = split(np.kron(np.eye(GROUP), basis[:, slots] * kept))
+    return bx_high, bx_low, back_high, back_low, by, flip(by), narrow_both, np.concatenate(wide)
 
 
 def signs(major, minor):
@@ -183,61 +186,55 @@
     count = NEAR * PART
     both = dot(jnp.concatenate([high, low], axis=0), high_ref[...], ((1,), (0,)))
     back = both[:count] + both[count:] + dot(high, low_ref[...], ((1,), (0,)))
-    back = low_slots(back, 1)
-    stacked = jnp.concatenate(
-        [spread[:, TILES * k : TILES * (k + 1)] for k in range(OWN)], axis=0
-    ).T
-    first = stacked.astype(BF16).astype(F32)
-    second = stacked - first
+    row = lax.broadcasted_iota(jnp.int32, (MODES, TILES * SLOTS), 0)
+    lane = lax.broadcasted_iota(jnp.int32, (MODES, TILES * SLOTS), 1)
+    target = TILES * (lane % SLOTS - KEPT) + lane // SLOTS
+    place = jnp.where(row == target, 1.0, 0.0).astype(BF16)
+    spreads = swap_rows(jnp.concatenate([spread] * NEAR, axis=0)).astype(BF16)
+    back = (low_slots(back, 1) + dot(spreads, place, ((1,), (0,)))).astype(BF16)
     for t in range(TILES):
         cols = slice(SLOTS * t, SLOTS * (t + 1))
-        rows = jnp.concatenate([back[PART * l : PART * (l + 1), cols] for l in range(GROUP)], axis=1)
-        extra = jnp.concatenate([first[t : t + 1], second[t : t + 1]], axis=0)
-        pieces = []
-        for k in range(NEAR):
-            pieces += [rows[GROUP * k : GROUP * (k + 1)], extra]
-        sent_ref[NEAR * CHUNK * t : NEAR * CHUNK * (t + 1), :] = jnp.concatenate(
-            pieces, axis=0
-        ).astype(BF16)
+        sent_ref[PART * t : PART * (t + 1), :] = jnp.concatenate(
+            [back[PART * l : PART * (l + 1), cols] for l in range(GROUP)], axis=1
+        )
 
 
 def apply_kernel(
-    states_ref, got_ref, by_ref, wide_ref, out_ref, spread_ref, back, filled, mixed, turned, variance, sems
+    states_ref, got_ref, by_ref, wide_ref, out_ref, spread_ref, back, filled, variance, sems
 ):
     def copy(c, h):
         part = (pl.ds(GROUP * c, GROUP), slice(None), pl.ds(HALF * h, HALF))
         return pltpu.make_async_copy(filled.at[part], out_ref.at[part], sems.at[2 * c + h])
 
-    for t in range(TILES):
-        rows = got_ref[NEAR * CHUNK * t : NEAR * CHUNK * (t + 1), :].astype(F32)
-        for k in range(NEAR):
-            row = SIDE * (k % 2) + 2 * t + k // 2
-            extra = rows[CHUNK * k + GROUP : CHUNK * (k + 1)]
-            mixed[row : row + 1, :] = extra[:1] + extra[1:]
-    turned[...] = mixed[...].T
-    for l in range(GROUP):
-        strips = [turned[pl.ds(GROUP * l + k, OWN, stride=PART), :] for k in range(GROUP)]
-        for c in range(2):
-            variance[GROUP * c + l] = jnp.concatenate(
-                [s[:, SIDE * c : SIDE * (c + 1)] for s in strips], axis=1
-            )
-    last = pltpu.make_async_copy(variance, spread_ref, sems.at[4])
-    last.start()
     sign = signs(SIDE, GROUP).astype(BF16)
     count = GROUP * ROWS
+    row = lax.broadcasted_iota(jnp.int32, (MODES, MODES), 0)
+    lane = lax.broadcasted_iota(jnp.int32, (MODES, MODES), 1)
+    order = jnp.where(lane == SIDE * (row % GROUP) + row // GROUP, 1.0, 0.0).astype(BF16)
     for c in range(2):
-        for t in range(TILES):
-            rows = got_ref[NEAR * CHUNK * t : NEAR * CHUNK * (t + 1), :].astype(F32)
+        for r in range(SIDE // 2):
+            rows = got_ref[4 * GROUP * r : 4 * GROUP * (r + 1), :].astype(F32)
             for k in range(2):
-                r, row = 2 * t + k, CHUNK * (2 * k + c)
-                back[c, GROUP * r : GROUP * (r + 1), :] = rows[row : row + GROUP]
-        both = dot(wide_ref[...], back[c].astype(BF16).T, ((1,), (0,)))
+                start = GROUP * (2 * k + c)
+                to = GROUP * (2 * r + k)
+                back[to : to + GROUP, :] = rows[start : start + GROUP]
+        slots = back[...].T
+        spreads = jnp.concatenate(
+            [slots[SLOTS * l + KEPT : SLOTS * (l + 1)] for l in range(GROUP)], axis=0
+        ).astype(BF16)
+        variance[GROUP * c : GROUP * (c + 1)] = dot(spreads, order, ((1,), (0,))).reshape(
+            GROUP, OWN, MODES
+        )
+        both = dot(wide_ref[...], slots.astype(BF16), ((1,), (0,)))
         modes = (both[:count] + both[count:]).astype(BF16)
         for h in range(2):
             cols = slice(HALF * h, HALF * (h + 1))
             increment = dot(modes if h == 0 else modes * sign, by_ref[...], ((1,), (0,)))
             field = states_ref[GROUP * c : GROUP * (c + 1), :, cols].astype(F32)
             total = field + increment.reshape(GROUP, ROWS, HALF)
+            if c == 1 and h == 0:
+                last = pltpu.make_async_copy(variance, spread_ref, sems.at[4])
+                last.start()
             filled[GROUP * c : GROUP * (c + 1), :, cols] = total.astype(BF16)
             copy(c, h).start()
     for c in range(2):
@@ -260,7 +257,7 @@
 
 
 def per_device(consts, states, obs_var, relax_rate):
-    bx_high, bx_low, bx_high_t, bx_low_t, by, by_t, narrow, widen = consts
+    bx_high, bx_low, back_high, back_low, by, by_t, narrow, widen = consts
     field = states[0]
     hbm = pl.BlockSpec(memory_space=pltpu.HBM)
     vmem = pl.BlockSpec(memory_space=pltpu.VMEM)
@@ -293,20 +290,18 @@
     gathered = lax.all_to_all(copies, "far", 0, 0, tiled=True)
     sent = call(
         nudge_kernel,
-        shape((devices * CHUNK, lanes), BF16),
+        shape((devices * GROUP, lanes), BF16),
         in_specs=[vmem] * 6,
         out_specs=vmem,
-    )(gathered, coeffs, obs_var[None], relax_rate[None], bx_high_t, bx_low_t)
+    )(gathered, coeffs, obs_var[None], relax_rate[None], back_high, back_low)
     nudged, spread = call(
         apply_kernel,
         (shape((LEVELS, ROWS, N), BF16), shape((LEVELS, OWN, MODES), F32)),
         in_specs=[vmem] * 4,
         out_specs=(hbm, hbm),
         scratch_shapes=[
-            pltpu.VMEM((2, MODES, lanes), F32),
+            pltpu.VMEM((MODES, lanes), F32),
             pltpu.VMEM((LEVELS, ROWS, N), BF16),
-            pltpu.VMEM((2 * SIDE, lanes), F32),
-            pltpu.VMEM((lanes, 2 * SIDE), F32),
             pltpu.VMEM((LEVELS, OWN, MODES), F32),
             pltpu.SemaphoreType.DMA((5,)),
         ],

time: 66.4 us -> 65.4 us (0.985)
  blocking collectives: 59.8 us -> 58.6 us
    all_to_all x2, blocking collectives: 50.1 us -> 49 us  [exchange(): lax.all_to_all(chunks, ('tile', 'near'), 0, 0, tiled=True)]
where the time goes in v7:
time: 65.4 us; the launch traced here: 65.2 us
  blocking collectives  58.6 us (90%)
  Pallas kernels  5.76 us (9%)
  between operations  0.74 us (1%)
    all_to_all x2, blocking collectives, exchange(): lax.all_to_all(chunks, ('tile', 'near'), 0, 0, tiled=True)  49 us
    all_to_all x1, blocking collectives, per_device(): gathered = lax.all_to_all(copies, 'far', 0, 0, tiled=True)  9.61 us
    pallas_call x1, Pallas kernels, per_device(): call(project_kernel, shape((devices * GROUP, lanes), BF16), in_specs=[hbm...  2.66 us
    pallas_call x1, Pallas kernels, per_device(): call(apply_kernel, (shape((LEVELS, ROWS, N), BF16), shape((LEVELS, OWN, M...  2.14 us

profile of v7, /device:TPU:1, one launch (start us, length us, event | category | flops | bytes accessed | tf_op | source)
XLA Modules:
  0.0 65.2 jit_solution(12597033300746238370)
XLA Ops:
  0.6 0.0 copy-start.3
  0.6 0.0 copy-start.4
  0.7 0.0 copy-start.1
  0.7 0.0 copy-start.2
  0.7 0.0 copy-start.7
  0.7 0.0 copy-start.8
  0.7 2.7 %shard_map.122 = bf16[512,128]{1,0:T(8,128)(2,1)S(1)} custom-call(bf16[8,64,2048]{2,1,0:T(8,128)(2,1)} %bitcast.8, bf16[1024,256]{1,0:T(8,128)(2,1)} %constant.16.clone.by_ref, bf16[256,256]{1,0:T(8,128)(2,1)} %constant.17.clone.narrow_ref), custom_call_target="tpu_custom_call" | custom-call | tf_op jit(solution)/shard_map/pallas_call | solution.py:270
  3.4 0.0 copy-start
  3.4 0.0 copy-start.5
  3.4 0.0 copy-start.6
  3.4 30.4 %all_to_all.15 = bf16[128,2,2,128]{3,2,1,0:T(2,128)(2,1)S(1)} all-to-all(bf16[128,2,2,128]{3,2,1,0:T(2,128)(2,1)S(1)} %bitcast.13), channel_id=1, replica_groups=mesh['far'=4,'near'=4,'tile'=32] {'tile','near'}, dimensions={0} | all-to-all | bytes 262144 | tf_op jit(solution)/shard_map/all_to_all | solution.py:268
  33.8 0.0 copy-done.3
  33.8 0.0 copy-done.4
  33.8 0.4 shard_map.123
  34.2 9.6 %all_to_all.16.all_ref = f32[4,64,256]{2,1,0:T(8,128)S(1)} all-to-all(f32[4,64,256]{2,1,0:T(8,128)S(1)} %get-tuple-element.6), channel_id=1, replica_groups=mesh['far'=4,'near'=4,'tile'=32] {'far'}, dimensions={0} | all-to-all | bytes 524288 | tf_op jit(solution)/shard_map/all_to_all | solution.py:290
  43.8 0.0 copy-done.1
  43.8 0.0 copy-done.2
  43.8 0.0 copy-done.7
  43.8 0.0 copy-done.8
  43.8 0.6 shard_map.124
  44.4 18.6 %all_to_all.17 = bf16[128,2,2,128]{3,2,1,0:T(2,128)(2,1)S(1)} all-to-all(bf16[128,2,2,128]{3,2,1,0:T(2,128)(2,1)S(1)} %bitcast.12), channel_id=1, replica_groups=mesh['far'=4,'near'=4,'tile'=32] {'tile','near'}, dimensions={0} | all-to-all | bytes 262144 | tf_op jit(solution)/shard_map/all_to_all | solution.py:268
  63.1 0.0 copy-done
  63.1 0.0 copy-done.5
  63.1 0.0 copy-done.6
  63.1 2.1 %shard_map.125 = (bf16[8,64,2048]{2,1,0:T(8,128)(2,1)}, f32[8,8,256]{2,1,0:T(8,128)}) custom-call(bf16[8,64,2048]{2,1,0:T(8,128)(2,1)S(1)} %bitcast.9, bf16[512,128]{1,0:T(8,128)(2,1)S(1)} %bitcast.11, bf16[256,1024]{1,0:T(8,128)(2,1)S(1)} %copy-done.5, bf16[512,128]{1,0:T(8,128)(2,1)S(1)} %copy-done.6), custom_call_target="tpu_custom_call" | custom-call | tf_op jit(solution)/shard_map/pallas_call | solution.py:297
Async XLA Ops:
  0.6 33.2 %copy-start.3 = (bf16[1024,256]{1,0:T(8,128)(2,1)S(1)}, bf16[1024,256]{1,0:T(8,128)(2,1)}, u32[]{:S(2)}) copy-start(bf16[1024,256]{1,0:T(8,128)(2,1)} %constant.19.clone.low_ref) | copy-start | bytes 1572868
  0.6 33.2 %copy-start.4 = (bf16[1024,256]{1,0:T(8,128)(2,1)S(1)}, bf16[1024,256]{1,0:T(8,128)(2,1)}, u32[]{:S(2)}) copy-start(bf16[1024,256]{1,0:T(8,128)(2,1)} %constant.18.clone.high_ref) | copy-start | bytes 1572868
  0.7 43.1 %copy-start.1 = (bf16[256,1024]{1,0:T(8,128)(2,1)S(1)}, bf16[256,1024]{1,0:T(8,128)(2,1)}, u32[]{:S(2)}) copy-start(bf16[256,1024]{1,0:T(8,128)(2,1)} %constant.21.clone.low_ref) | copy-start | bytes 1572868
  0.7 43.1 %copy-start.2 = (bf16[256,1024]{1,0:T(8,128)(2,1)S(1)}, bf16[256,1024]{1,0:T(8,128)(2,1)}, u32[]{:S(2)}) copy-start(bf16[256,1024]{1,0:T(8,128)(2,1)} %constant.20.clone.high_ref) | copy-start | bytes 1572868
  0.7 43.1 %copy-start.7 = (f32[8]{0:T(128)S(1)}, f32[8]{0:T(128)}, u32[]{:S(2)}) copy-start(f32[8]{0:T(128)} %param.12) | copy-start | bytes 100
  0.7 43.1 %copy-start.8 = (f32[8]{0:T(128)S(1)}, f32[8]{0:T(128)}, u32[]{:S(2)}) copy-start(f32[8]{0:T(128)} %param.13) | copy-start | bytes 100
  3.4 59.7 %copy-start = (bf16[1,8,64,2048]{3,2,1,0:T(8,128)(2,1)S(1)}, bf16[1,8,64,2048]{3,2,1,0:T(8,128)(2,1)}, u32[]{:S(2)}) copy-start(bf16[1,8,64,2048]{3,2,1,0:T(8,128)(2,1)} %param.11) | copy-start | bytes 6291460
  3.4 59.7 %copy-start.5 = (bf16[256,1024]{1,0:T(8,128)(2,1)S(1)}, bf16[256,1024]{1,0:T(8,128)(2,1)}, u32[]{:S(2)}) copy-start(bf16[256,1024]{1,0:T(8,128)(2,1)} %constant.22.clone.by_ref) | copy-start | bytes 1572868
  3.4 59.7 %copy-start.6 = (bf16[512,128]{1,0:T(8,128)(2,1)S(1)}, bf16[512,128]{1,0:T(8,128)(2,1)}, u32[]{:S(2)}) copy-start(bf16[512,128]{1,0:T(8,128)(2,1)} %constant.23.clone.wide_ref) | copy-start | bytes 393220

commit v8 on v7

--- a/solution.py
+++ b/solution.py
@@ -68,14 +68,12 @@
     )
     bx_high, bx_low = split(modes[:, slots][:, :, first].reshape(TILES * SLOTS, MODES))
     kept = (np.arange(SLOTS) < KEPT).astype(np.float64)
-    returned = (modes[:, slots] * kept[:, None])[:, :, first].reshape(TILES * SLOTS, MODES)
-    back_high, back_low = split(flip(returned))
     narrow = np.kron(np.eye(GROUP), basis[:, slots].T)
     narrow_high, narrow_low = split(narrow)
     by = full[:HALF].astype(np.float32).astype(BF16)[:, second]
     narrow_both = np.concatenate([narrow_high, narrow_low], axis=0)
     wide = split(np.kron(np.eye(GROUP), basis[:, slots] * kept))
-    return bx_high, bx_low, back_high, back_low, by, flip(by), narrow_both, np.concatenate(wide)
+    return bx_high, bx_low, by, flip(by), narrow_both, np.concatenate(wide)
 
 
 def signs(major, minor):
@@ -184,14 +182,16 @@
     misfit = jnp.concatenate([-gain * (own_ref[m, :] - driver) for m in members], axis=0)
     high, low = parts(swap_rows(misfit))
     count = NEAR * PART
-    both = dot(jnp.concatenate([high, low], axis=0), high_ref[...], ((1,), (0,)))
-    back = both[:count] + both[count:] + dot(high, low_ref[...], ((1,), (0,)))
+    both = dot(jnp.concatenate([high, low], axis=0), high_ref[...], ((1,), (1,)))
+    back = both[:count] + both[count:] + dot(high, low_ref[...], ((1,), (1,)))
     row = lax.broadcasted_iota(jnp.int32, (MODES, TILES * SLOTS), 0)
     lane = lax.broadcasted_iota(jnp.int32, (MODES, TILES * SLOTS), 1)
     target = TILES * (lane % SLOTS - KEPT) + lane // SLOTS
     place = jnp.where(row == target, 1.0, 0.0).astype(BF16)
     spreads = swap_rows(jnp.concatenate([spread] * NEAR, axis=0)).astype(BF16)
-    back = (low_slots(back, 1) + dot(spreads, place, ((1,), (0,)))).astype(BF16)
+    slot = lax.broadcasted_iota(jnp.int32, back.shape, 1) % SLOTS
+    placed = dot(spreads, place, ((1,), (0,)))
+    back = jnp.where(slot < KEPT, low_slots(back, 1), placed).astype(BF16)
     for t in range(TILES):
         cols = slice(SLOTS * t, SLOTS * (t + 1))
         sent_ref[PART * t : PART * (t + 1), :] = jnp.concatenate(
@@ -257,7 +257,7 @@
 
 
 def per_device(consts, states, obs_var, relax_rate):
-    bx_high, bx_low, back_high, back_low, by, by_t, narrow, widen = consts
+    bx_high, bx_low, by, by_t, narrow, widen = consts
     field = states[0]
     hbm = pl.BlockSpec(memory_space=pltpu.HBM)
     vmem = pl.BlockSpec(memory_space=pltpu.VMEM)
@@ -293,7 +293,7 @@
         shape((devices * GROUP, lanes), BF16),
         in_specs=[vmem] * 6,
         out_specs=vmem,
-    )(gathered, coeffs, obs_var[None], relax_rate[None], back_high, back_low)
+    )(gathered, coeffs, obs_var[None], relax_rate[None], bx_high, bx_low)
     nudged, spread = call(
         apply_kernel,
         (shape((LEVELS, ROWS, N), BF16), shape((LEVELS, OWN, MODES), F32)),

time: 65.4 us -> 65.5 us (level)
  no operation moved by 1% of the time
where the time goes in v8:
time: 65.5 us; the launch traced here: 65.3 us
  blocking collectives  58.6 us (89%)
  Pallas kernels  5.87 us (9%)
  between operations  0.72 us (1%)
    all_to_all x2, blocking collectives, exchange(): lax.all_to_all(chunks, ('tile', 'near'), 0, 0, tiled=True)  49 us
    all_to_all x1, blocking collectives, per_device(): gathered = lax.all_to_all(copies, 'far', 0, 0, tiled=True)  9.61 us
    pallas_call x1, Pallas kernels, per_device(): call(project_kernel, shape((devices * GROUP, lanes), BF16), in_specs=[hbm...  2.61 us
    pallas_call x1, Pallas kernels, per_device(): call(apply_kernel, (shape((LEVELS, ROWS, N), BF16), shape((LEVELS, OWN, M...  2.14 us

profile of v8, /device:TPU:1, one launch (start us, length us, event | category | flops | bytes accessed | tf_op | source)
XLA Modules:
  0.0 65.3 jit_solution(2787778072028395844)
XLA Ops:
  0.6 0.0 copy-start.1
  0.6 0.0 copy-start.2
  0.7 0.0 copy-start.5
  0.7 0.0 copy-start.6
  0.7 2.6 %shard_map.104 = bf16[512,128]{1,0:T(8,128)(2,1)S(1)} custom-call(bf16[8,64,2048]{2,1,0:T(8,128)(2,1)} %bitcast.8, bf16[1024,256]{1,0:T(8,128)(2,1)} %constant.12.clone.by_ref, bf16[256,256]{1,0:T(8,128)(2,1)} %constant.13.clone.narrow_ref), custom_call_target="tpu_custom_call" | custom-call | tf_op jit(solution)/shard_map/pallas_call | solution.py:270
  3.3 0.0 copy-start
  3.3 0.0 copy-start.3
  3.3 0.0 copy-start.4
  3.3 30.4 %all_to_all.15 = bf16[128,2,2,128]{3,2,1,0:T(2,128)(2,1)S(1)} all-to-all(bf16[128,2,2,128]{3,2,1,0:T(2,128)(2,1)S(1)} %bitcast.13), channel_id=1, replica_groups=mesh['far'=4,'near'=4,'tile'=32] {'tile','near'}, dimensions={0} | all-to-all | bytes 262144 | tf_op jit(solution)/shard_map/all_to_all | solution.py:268
  33.7 0.0 copy-done.1
  33.7 0.0 copy-done.2
  33.7 0.4 shard_map.105
  34.1 9.6 %all_to_all.16.all_ref = f32[4,64,256]{2,1,0:T(8,128)S(1)} all-to-all(f32[4,64,256]{2,1,0:T(8,128)S(1)} %get-tuple-element.6), channel_id=1, replica_groups=mesh['far'=4,'near'=4,'tile'=32] {'far'}, dimensions={0} | all-to-all | bytes 524288 | tf_op jit(solution)/shard_map/all_to_all | solution.py:290
  43.7 0.0 copy-done.5
  43.7 0.0 copy-done.6
  43.7 0.7 %shard_map.106 = bf16[512,128]{1,0:T(8,128)(2,1)S(1)} custom-call(f32[4,64,256]{2,1,0:T(8,128)S(1)} %all_to_all.16.all_ref, f32[64,256]{1,0:T(8,128)S(1)} %get-tuple-element.7.own_ref, f32[1,8]{1,0:T(1,128)S(1)} %bitcast.14, f32[1,8]{1,0:T(1,128)S(1)} %bitcast.15, bf16[1024,256]{1,0:T(8,128)(2,1)S(1)} %copy-done.2, bf16[1024,256]{1,0:T(8,128)(2,1)S(1)} %copy-done.1), custom_call_target="tpu_custom_call" | custom-call | tf_op jit(solution)/shard_map/pallas_call | solution.py:291
  44.5 18.6 %all_to_all.17 = bf16[128,2,2,128]{3,2,1,0:T(2,128)(2,1)S(1)} all-to-all(bf16[128,2,2,128]{3,2,1,0:T(2,128)(2,1)S(1)} %bitcast.11), channel_id=1, replica_groups=mesh['far'=4,'near'=4,'tile'=32] {'tile','near'}, dimensions={0} | all-to-all | bytes 262144 | tf_op jit(solution)/shard_map/all_to_all | solution.py:268
  63.1 0.0 copy-done
  63.1 0.0 copy-done.3
  63.1 0.0 copy-done.4
  63.1 2.1 %shard_map.107 = (bf16[8,64,2048]{2,1,0:T(8,128)(2,1)}, f32[8,8,256]{2,1,0:T(8,128)}) custom-call(bf16[8,64,2048]{2,1,0:T(8,128)(2,1)S(1)} %bitcast.9, bf16[512,128]{1,0:T(8,128)(2,1)S(1)} %bitcast.10, bf16[256,1024]{1,0:T(8,128)(2,1)S(1)} %copy-done.3, bf16[512,128]{1,0:T(8,128)(2,1)S(1)} %copy-done.4), custom_call_target="tpu_custom_call" | custom-call | tf_op jit(solution)/shard_map/pallas_call | solution.py:297
Async XLA Ops:
  0.6 33.1 %copy-start.1 = (bf16[1024,256]{1,0:T(8,128)(2,1)S(1)}, bf16[1024,256]{1,0:T(8,128)(2,1)}, u32[]{:S(2)}) copy-start(bf16[1024,256]{1,0:T(8,128)(2,1)} %constant.15.clone.low_ref) | copy-start | bytes 1572868
  0.6 33.1 %copy-start.2 = (bf16[1024,256]{1,0:T(8,128)(2,1)S(1)}, bf16[1024,256]{1,0:T(8,128)(2,1)}, u32[]{:S(2)}) copy-start(bf16[1024,256]{1,0:T(8,128)(2,1)} %constant.14.clone.high_ref) | copy-start | bytes 1572868
  0.7 43.1 %copy-start.5 = (f32[8]{0:T(128)S(1)}, f32[8]{0:T(128)}, u32[]{:S(2)}) copy-start(f32[8]{0:T(128)} %param.10) | copy-start | bytes 100
  0.7 43.1 %copy-start.6 = (f32[8]{0:T(128)S(1)}, f32[8]{0:T(128)}, u32[]{:S(2)}) copy-start(f32[8]{0:T(128)} %param.11) | copy-start | bytes 100
  3.3 59.8 %copy-start = (bf16[1,8,64,2048]{3,2,1,0:T(8,128)(2,1)S(1)}, bf16[1,8,64,2048]{3,2,1,0:T(8,128)(2,1)}, u32[]{:S(2)}) copy-start(bf16[1,8,64,2048]{3,2,1,0:T(8,128)(2,1)} %param.9) | copy-start | bytes 6291460
  3.3 59.8 %copy-start.3 = (bf16[256,1024]{1,0:T(8,128)(2,1)S(1)}, bf16[256,1024]{1,0:T(8,128)(2,1)}, u32[]{:S(2)}) copy-start(bf16[256,1024]{1,0:T(8,128)(2,1)} %constant.16.clone.by_ref) | copy-start | bytes 1572868
  3.3 59.8 %copy-start.4 = (bf16[512,128]{1,0:T(8,128)(2,1)S(1)}, bf16[512,128]{1,0:T(8,128)(2,1)}, u32[]{:S(2)}) copy-start(bf16[512,128]{1,0:T(8,128)(2,1)} %constant.17.clone.wide_ref) | copy-start | bytes 393220
